TPU v7x, 8 devices: a whole 2x2x1 slice. The times are simulated.
8 devices in a mesh: sweep: 1 (over z), ent: 8 (over y, x, core).
Axes of the slice: x: 2, y: 2, z: 1, core: 2. Of those that a mesh axis runs over, the one named last changes fastest.
Arguments:
- ent_table: float32 [65536, 400], P(('sweep', 'ent'))
- ada_state: float32 [65536], P(('sweep', 'ent'))
- rel_table: float32 [237, 400], P('sweep')
- head_idx: int32 [8, 6, 1024], P(('sweep', 'ent'))
- tail_idx: int32 [8, 6, 1024], P(('sweep', 'ent'))
- rel_idx: int32 [8, 6, 1024], P(('sweep', 'ent'))
- neg_idx: int32 [8, 6, 256], P(('sweep', 'ent'))
- edge_mask: int32 [8, 6, 1024], P(('sweep', 'ent'))
Outputs:
- output 1: float32 [65536, 400], P(('sweep', 'ent'))
- output 2: float32 [65536], P(('sweep', 'ent'))
- output 3: float32 [237, 400], P('sweep')
- output 4: float32 [8, 6], P(('sweep', 'ent'))
All inputs are finite; a program needn't handle non-finite values.
Results may differ from a plain program's by a relative error of at most 0.00260891.
Values are sent between devices in bfloat16 or wider.
A program may use at most 1 GiB of HBM per device.

v0:
```python
import jax
import jax.numpy as jnp
from jax import lax
from jax.sharding import PartitionSpec as P

LEARN_RATE = 0.25
ADA_EPS = 1e-10


def bucket_grads(head_rows, tail_bf, neg_bf, rel_rows, weight):
    emb_dim = head_rows.shape[1]
    half_dim = emb_dim // 2
    score_scale = emb_dim ** -0.5
    h_re = head_rows[:, :half_dim]
    h_im = head_rows[:, half_dim:]
    r_re = rel_rows[:, :half_dim]
    r_im = rel_rows[:, half_dim:]
    query = jnp.concatenate([h_re * r_re - h_im * r_im, h_re * r_im + h_im * r_re], axis=1)
    query_bf = query.astype(jnp.bfloat16)
    tail_rows = tail_bf.astype(jnp.float32)
    pos_score = score_scale * jnp.sum(query * tail_rows, axis=1)
    neg_score = score_scale * lax.dot_general(query_bf, neg_bf, (((1,), (1,)), ((), ())), preferred_element_type=jnp.float32)
    top_score = jnp.maximum(pos_score, jnp.max(neg_score, axis=1))
    pos_exp = jnp.exp(pos_score - top_score)
    neg_exp = jnp.exp(neg_score - top_score[:, None])
    denom_sum = pos_exp + jnp.sum(neg_exp, axis=1)
    weight_f = weight.astype(jnp.float32)
    loss_sum = jnp.sum(weight_f * (top_score + jnp.log(denom_sum) - pos_score))
    d_pos = weight_f * (pos_exp / denom_sum - 1.0)
    d_negs = ((weight_f / denom_sum)[:, None] * neg_exp).astype(jnp.bfloat16)
    d_query = score_scale * (d_pos[:, None] * tail_rows + jnp.dot(d_negs, neg_bf, preferred_element_type=jnp.float32))
    d_tail = score_scale * d_pos[:, None] * query
    d_neg = score_scale * lax.dot_general(d_negs, query_bf, (((0,), (0,)), ((), ())), preferred_element_type=jnp.float32)
    dq_re = d_query[:, :half_dim]
    dq_im = d_query[:, half_dim:]
    d_head = jnp.concatenate([dq_re * r_re + dq_im * r_im, dq_im * r_re - dq_re * r_im], axis=1)
    d_rel = jnp.concatenate([dq_re * h_re + dq_im * h_im, dq_im * h_re - dq_re * h_im], axis=1)
    return loss_sum, d_head, d_tail, d_neg, d_rel


def adagrad_rows(table, state, row_grad):
    new_state = state + jnp.mean(row_grad * row_grad, axis=1)
    new_table = table - LEARN_RATE * row_grad / jnp.sqrt(new_state + ADA_EPS)[:, None]
    return new_table, new_state


def solution(mesh):
    ent_devs = mesh.shape['ent']
    row_spec = P(('sweep', 'ent'), None)
    state_spec = P(('sweep', 'ent'))
    rel_spec = P('sweep', None)
    edge_spec = P(('sweep', 'ent'), None, None)

    def per_device(ent_part, ada_part, rel_table, head_idx, tail_idx, rel_idx, neg_idx, edge_mask):
        part_rows = ent_part.shape[0]
        rel_count = rel_table.shape[0]
        rounds = head_idx.shape[1]
        edge_count = head_idx.shape[2]
        rel_acc = jnp.zeros((rel_count,), jnp.float32)
        loss_list = []
        for step in range(rounds):
            shift = step + 1
            to_owner = [(sender, (sender + shift) % ent_devs) for sender in range(ent_devs)]
            to_asker = [(target, sender) for sender, target in to_owner]
            head_ids = head_idx[0, step]
            rel_ids = rel_idx[0, step]
            wanted = jnp.concatenate([tail_idx[0, step], neg_idx[0, step]])
            served = lax.ppermute(wanted, 'ent', to_owner)
            fetched = lax.ppermute(ent_part[served].astype(jnp.bfloat16), 'ent', to_asker)
            loss_sum, d_head, d_tail, d_neg, d_rel = bucket_grads(ent_part[head_ids], fetched[:edge_count], fetched[edge_count:], rel_table[rel_ids], edge_mask[0, step])
            returned = lax.ppermute(jnp.concatenate([d_tail, d_neg]), 'ent', to_owner)
            row_grad = jax.ops.segment_sum(jnp.concatenate([d_head, returned]), jnp.concatenate([head_ids, served]), num_segments=part_rows)
            rel_grad = lax.psum(jax.ops.segment_sum(d_rel, rel_ids, num_segments=rel_count), 'ent')
            ent_part, ada_part = adagrad_rows(ent_part, ada_part, row_grad)
            rel_table, rel_acc = adagrad_rows(rel_table, rel_acc, rel_grad)
            loss_list.append(loss_sum / edge_count)
        return ent_part, ada_part, rel_table, jnp.stack(loss_list)[None, :]

    return jax.shard_map(per_device, mesh=mesh, in_specs=(row_spec, state_spec, rel_spec, edge_spec, edge_spec, edge_spec, edge_spec, edge_spec), out_specs=(row_spec, state_spec, rel_spec, row_spec), check_vma=False)
```

profile of v0, /device:TPU:1, one launch (start us, length us, event | category | flops | bytes accessed | tf_op | source)
XLA Modules:
  0.0 1091.8 jit_solution(7508854999040927344)
XLA Ops:
  18.8 15.9 %copy.58 = f32[8192,400]{1,0:T(8,128)} copy(f32[8192,400]{0,1:T(8,128)} %param.8) | data formatting | bytes 26214400 | tf_op args[0]
  34.7 9.8 gather_fusion
  50.6 10.5 gather_fusion.2
  92.5 8.1 scatter_custom_fusion.1
  100.9 42.6 %all-reduce.7.cloned.1.call-done = f32[237,400]{1,0:T(8,128)} async-done(((f32[237,400]{1,0:T(8,128)}), f32[237,400]{1,0:T(8,128)}) %all-reduce.7.cloned.1.call-update) | async-done | bytes 379216 | tf_op jit(solution)/shard_map/psum | solution.py:73
  148.3 5.6 copy.57
  153.9 23.0 %scatter_custom_fusion = f32[8192,400]{1,0:T(8,128)} fusion(s32[2304]{0:T(1024)S(1)} %pad_add_fusion, f32[2304,400]{1,0:T(8,128)} %copy.57, f32[]{:T(128)} %constant.46.clone.1), kind=kCustom, calls=%fused_computation.52 | custom fusion | flops 921600 | bytes 13107712 | tf_op jit(solution)/shard_map/scatter-add | solution.py:72
  176.9 7.1 multiply_reduce_fusion.5
  184.0 17.9 %divide_subtract_fusion.5 = f32[8192,400]{1,0:T(8,128)} fusion(f32[8192,400]{1,0:T(8,128)} %copy.58, f32[8192,400]{1,0:T(8,128)} %scatter_custom_fusion, f32[8192]{0:T(1024)S(1)} %add_sqrt_fusion.5), kind=kLoop, calls=%fused_computation.40 | loop fusion | flops 9830400 | bytes 39354368 | tf_op jit(solution)/shard_map/sub | solution.py:43
  201.9 9.9 gather_fusion.5
  222.7 9.8 gather_fusion.3
  253.7 8.5 scatter_custom_fusion.3
  262.4 63.4 %all-reduce.9.cloned.1.call-done = f32[237,400]{1,0:T(8,128)} async-done(((f32[237,400]{1,0:T(8,128)}), f32[237,400]{1,0:T(8,128)}) %all-reduce.9.cloned.1.call-update) | async-done | bytes 379216 | tf_op jit(solution)/shard_map/psum | solution.py:73
  330.6 5.6 copy.66
  336.2 23.1 %scatter_custom_fusion.2 = f32[8192,400]{1,0:T(8,128)} fusion(s32[2304]{0:T(1024)S(1)} %pad_add_fusion.1, f32[2304,400]{1,0:T(8,128)} %copy.66, f32[]{:T(128)} %constant.46.clone.1), kind=kCustom, calls=%fused_computation.50 | custom fusion | flops 921600 | bytes 13107712 | tf_op jit(solution)/shard_map/scatter-add | solution.py:72
  359.3 7.1 multiply_reduce_fusion.4
  366.4 17.9 %divide_subtract_fusion.4 = f32[8192,400]{1,0:T(8,128)} fusion(f32[8192,400]{1,0:T(8,128)} %divide_subtract_fusion.5, f32[8192,400]{1,0:T(8,128)} %scatter_custom_fusion.2, f32[8192]{0:T(1024)S(1)} %get-tuple-element.26), kind=kLoop, calls=%fused_computation.38 | loop fusion | flops 9830400 | bytes 39354368 | tf_op jit(solution)/shard_map/sub | solution.py:43
  384.3 9.9 gather_fusion.8
  407.4 11.0 %gather_fusion.6 = f32[1024,400]{1,0:T(8,128)} fusion(f32[8192,400]{1,0:T(8,128)} %divide_subtract_fusion.4, s32[1024]{0:T(1024)S(1)} %copy-done.42), kind=kCustom, calls=%fused_computation.6 | custom fusion | bytes 3280896 | tf_op jit(solution)/shard_map/gather | solution.py:70
  439.7 8.1 scatter_custom_fusion.5
  448.4 46.7 %all-reduce.11.cloned.1.call-done = f32[237,400]{1,0:T(8,128)} async-done(((f32[237,400]{1,0:T(8,128)}), f32[237,400]{1,0:T(8,128)}) %all-reduce.11.cloned.1.call-update) | async-done | bytes 379216 | tf_op jit(solution)/shard_map/psum | solution.py:73
  499.9 5.6 copy.73
  505.5 23.0 %scatter_custom_fusion.4 = f32[8192,400]{1,0:T(8,128)} fusion(s32[2304]{0:T(1024)S(1)} %pad_add_fusion.2, f32[2304,400]{1,0:T(8,128)} %copy.73, f32[]{:T(128)} %constant.46.clone.1), kind=kCustom, calls=%fused_computation.48 | custom fusion | flops 921600 | bytes 13107712 | tf_op jit(solution)/shard_map/scatter-add | solution.py:72
  528.5 7.1 multiply_reduce_fusion.3
  535.6 17.9 %divide_subtract_fusion.3 = f32[8192,400]{1,0:T(8,128)} fusion(f32[8192,400]{1,0:T(8,128)} %divide_subtract_fusion.4, f32[8192,400]{1,0:T(8,128)} %scatter_custom_fusion.4, f32[8192]{0:T(1024)S(1)} %add_sqrt_fusion.3), kind=kLoop, calls=%fused_computation.36 | loop fusion | flops 9830400 | bytes 39354368 | tf_op jit(solution)/shard_map/sub | solution.py:43
  553.5 9.9 gather_fusion.11
  573.3 9.8 gather_fusion.9
  603.8 8.2 scatter_custom_fusion.7
  612.8 43.9 %all-reduce.13.cloned.1.call-done = f32[237,400]{1,0:T(8,128)} async-done(((f32[237,400]{1,0:T(8,128)}), f32[237,400]{1,0:T(8,128)}) %all-reduce.13.cloned.1.call-update) | async-done | bytes 379216 | tf_op jit(solution)/shard_map/psum | solution.py:73
  667.2 23.3 %scatter_custom_fusion.6 = f32[8192,400]{1,0:T(8,128)} fusion(s32[2304]{0:T(1024)S(1)} %pad_add_fusion.3, f32[2304,400]{1,0:T(8,128)} %copy.80, f32[]{:T(128)} %constant.46.clone.1), kind=kCustom, calls=%fused_computation.46 | custom fusion | flops 921600 | bytes 13107712 | tf_op jit(solution)/shard_map/scatter-add | solution.py:72
  690.5 7.1 multiply_reduce_fusion.2
  697.6 17.9 %divide_subtract_fusion.2 = f32[8192,400]{1,0:T(8,128)} fusion(f32[8192,400]{1,0:T(8,128)} %divide_subtract_fusion.3, f32[8192,400]{1,0:T(8,128)} %scatter_custom_fusion.6, f32[8192]{0:T(1024)S(1)} %get-tuple-element.20), kind=kLoop, calls=%fused_computation.34 | loop fusion | flops 9830400 | bytes 39354368 | tf_op jit(solution)/shard_map/sub | solution.py:43
  715.5 9.9 gather_fusion.14
  737.9 9.8 gather_fusion.12
  768.0 8.2 scatter_custom_fusion.9
  777.1 46.2 %all-reduce.15.cloned.1.call-done = f32[237,400]{1,0:T(8,128)} async-done(((f32[237,400]{1,0:T(8,128)}), f32[237,400]{1,0:T(8,128)}) %all-reduce.15.cloned.1.call-update) | async-done | bytes 379216 | tf_op jit(solution)/shard_map/psum | solution.py:73
  833.7 23.0 %scatter_custom_fusion.8 = f32[8192,400]{1,0:T(8,128)} fusion(s32[2304]{0:T(1024)S(1)} %pad_add_fusion.4, f32[2304,400]{1,0:T(8,128)} %copy.87, f32[]{:T(128)} %constant.46.clone.1), kind=kCustom, calls=%fused_computation.44 | custom fusion | flops 921600 | bytes 13107712 | tf_op jit(solution)/shard_map/scatter-add | solution.py:72
  856.7 7.1 multiply_reduce_fusion.1
  863.8 17.9 %divide_subtract_fusion.1 = f32[8192,400]{1,0:T(8,128)} fusion(f32[8192,400]{1,0:T(8,128)} %divide_subtract_fusion.2, f32[8192,400]{1,0:T(8,128)} %scatter_custom_fusion.8, f32[8192]{0:T(1024)S(1)} %add_sqrt_fusion.1), kind=kLoop, calls=%fused_computation.32 | loop fusion | flops 9830400 | bytes 39354368 | tf_op jit(solution)/shard_map/sub | solution.py:43
  881.7 9.9 gather_fusion.17
  901.5 9.8 gather_fusion.15
  932.1 8.3 scatter_custom_fusion.11
  945.7 61.7 %all-reduce.17.cloned.1.call-done = f32[237,400]{1,0:T(8,128)} async-done(((f32[237,400]{1,0:T(8,128)}), f32[237,400]{1,0:T(8,128)}) %all-reduce.17.cloned.1.call-update) | async-done | bytes 379216 | tf_op jit(solution)/shard_map/psum | solution.py:73
  1014.3 5.6 copy.94
  1019.9 23.0 %scatter_custom_fusion.10 = f32[8192,400]{1,0:T(8,128)} fusion(s32[2304]{0:T(1024)S(1)} %pad_add_fusion.5, f32[2304,400]{1,0:T(8,128)} %copy.94, f32[]{:T(128)} %constant.46.clone.1), kind=kCustom, calls=%fused_computation.42 | custom fusion | flops 921600 | bytes 13107712 | tf_op jit(solution)/shard_map/scatter-add | solution.py:72
  1042.8 7.1 multiply_reduce_fusion
  1050.5 17.9 %divide_subtract_fusion = f32[8192,400]{1,0:T(8,128)} fusion(f32[8192,400]{1,0:T(8,128)} %divide_subtract_fusion.1, f32[8192,400]{1,0:T(8,128)} %scatter_custom_fusion.10, f32[8192]{0:T(1024)S(1)} %get-tuple-element.12), kind=kLoop, calls=%fused_computation.30 | loop fusion | flops 9830400 | bytes 39354368 | tf_op jit(solution)/shard_map/sub | solution.py:43
  1068.4 16.2 %copy.96 = f32[8192,400]{0,1:T(8,128)} copy(f32[8192,400]{1,0:T(8,128)} %divide_subtract_fusion) | data formatting | bytes 26214400
  (376 shorter events, 255.2 us)
Async XLA Ops:
  7.2 136.3 %all-reduce.7.cloned.1.call-start = ((), (), s32[]{:S(2)}) async-start(), calls=%async_computation | async-start | bytes 983040 | tf_op jit(solution)/shard_map/psum | solution.py:73
  8.8 41.8 %collective-permute-start = (s32[1280]{0:T(1024)S(1)}, s32[1280]{0:T(1024)S(1)}, u32[]{:S(2)}, u32[]{:S(2)}) collective-permute-start(s32[1280]{0:T(1024)S(1)} %pad_add_fusion.6), channel_id=1, source_target_pairs={{0,1},{1,2},{2,3},{3,4},{4,5},{5,6},{6,7},{7,0}} | collective-permute-start | bytes 15368 | tf_op jit(solution)/shard_map/ppermute | solution.py:68
  11.4 73.2 %collective-permute-start.3 = (s32[1280]{0:T(1024)S(1)}, s32[1280]{0:T(1024)S(1)}, u32[]{:S(2)}, u32[]{:S(2)}) collective-permute-start(s32[1280]{0:T(1024)S(1)} %pad_add_fusion.7), channel_id=1, source_target_pairs={{0,2},{1,3},{2,4},{3,5},{4,6},{5,7},{6,0},{7,1}} | collective-permute-start | bytes 15368 | tf_op jit(solution)/shard_map/ppermute | solution.py:68
  13.2 234.9 %collective-permute-start.6 = (s32[1280]{0:T(1024)}, s32[1280]{0:T(1024)S(1)}, u32[]{:S(2)}, u32[]{:S(2)}) collective-permute-start(s32[1280]{0:T(1024)} %pad_add_fusion.8), channel_id=1, source_target_pairs={{0,3},{1,4},{2,5},{3,6},{4,7},{5,0},{6,1},{7,2}} | collective-permute-start | bytes 15368 | tf_op jit(solution)/shard_map/ppermute | solution.py:68
  14.1 419.2 %collective-permute-start.9 = (s32[1280]{0:T(1024)}, s32[1280]{0:T(1024)}, u32[]{:S(2)}, u32[]{:S(2)}) collective-permute-start(s32[1280]{0:T(1024)} %pad_add_fusion.9), channel_id=1, source_target_pairs={{0,4},{1,5},{2,6},{3,7},{4,0},{5,1},{6,2},{7,3}} | collective-permute-start | bytes 15368 | tf_op jit(solution)/shard_map/ppermute | solution.py:68
  15.0 582.5 %collective-permute-start.12 = (s32[1280]{0:T(1024)}, s32[1280]{0:T(1024)}, u32[]{:S(2)}, u32[]{:S(2)}) collective-permute-start(s32[1280]{0:T(1024)} %pad_add_fusion.10), channel_id=1, source_target_pairs={{0,5},{1,6},{2,7},{3,0},{4,1},{5,2},{6,3},{7,4}} | collective-permute-start | bytes 15368 | tf_op jit(solution)/shard_map/ppermute | solution.py:68
  63.5 14.0 %collective-permute-start.1 = (bf16[1280,400]{0,1:T(8,128)(2,1)}, bf16[1280,400]{0,1:T(8,128)(2,1)}, u32[]{:S(2)}, u32[]{:S(2)}) collective-permute-start(bf16[1280,400]{0,1:T(8,128)(2,1)} %copy.56), channel_id=1, source_target_pairs={{1,0},{2,1},{3,2},{4,3},{5,4},{6,5},{7,6},{0,7}} | collective-permute-start | bytes 3072008 | tf_op jit(solution)/shard_map/ppermute | solution.py:69
  67.2 4.6 copy-start.41
  83.3 5.3 copy-start
  83.3 61.4 %collective-permute-start.2 = (f32[1280,400]{0,1:T(8,128)}, f32[1280,400]{0,1:T(8,128)}, u32[]{:S(2)}, u32[]{:S(2)}) collective-permute-start(f32[1280,400]{0,1:T(8,128)} %pad_maximum_fusion.6), channel_id=1, source_target_pairs={{0,1},{1,2},{2,3},{3,4},{4,5},{5,6},{6,7},{7,0}} | collective-permute-start | bytes 6144008 | tf_op jit(solution)/shard_map/ppermute | solution.py:71
  84.6 677.1 %collective-permute-start.15 = (s32[1280]{0:T(1024)}, s32[1280]{0:T(1024)}, u32[]{:S(2)}, u32[]{:S(2)}) collective-permute-start(s32[1280]{0:T(1024)} %pad_add_fusion.11), channel_id=1, source_target_pairs={{0,6},{1,7},{2,0},{3,1},{4,2},{5,3},{6,4},{7,5}} | collective-permute-start | bytes 15368 | tf_op jit(solution)/shard_map/ppermute | solution.py:68
  90.7 54.0 %copy-start.23 = (f32[1024,200]{0,1:T(8,128)S(1)}, f32[1024,200]{0,1:T(8,128)}, u32[]{:S(2)}) copy-start(f32[1024,200]{0,1:T(8,128)} %get-tuple-element.102) | copy-start | bytes 2457604
  92.5 52.2 %copy-start.24 = (f32[1024,200]{0,1:T(8,128)S(1)}, f32[1024,200]{0,1:T(8,128)}, u32[]{:S(2)}) copy-start(f32[1024,200]{0,1:T(8,128)} %get-tuple-element.103) | copy-start | bytes 2457604
  100.7 225.1 %all-reduce.9.cloned.1.call-start = ((), (), s32[]{:S(2)}) async-start(), calls=%async_computation.1 | async-start | bytes 983040 | tf_op jit(solution)/shard_map/psum | solution.py:73
  176.9 7.1 copy-start.35
  213.3 26.4 %collective-permute-start.4 = (bf16[1280,400]{0,1:T(8,128)(2,1)}, bf16[1280,400]{0,1:T(8,128)(2,1)}, u32[]{:S(2)}, u32[]{:S(2)}) collective-permute-start(bf16[1280,400]{0,1:T(8,128)(2,1)} %copy.65), channel_id=1, source_target_pairs={{2,0},{3,1},{4,2},{5,3},{6,4},{7,5},{0,6},{1,7}} | collective-permute-start | bytes 3072008 | tf_op jit(solution)/shard_map/ppermute | solution.py:69
  234.1 4.1 copy-start.4
  245.7 81.3 %collective-permute-start.5 = (f32[1280,400]{0,1:T(8,128)}, f32[1280,400]{0,1:T(8,128)}, u32[]{:S(2)}, u32[]{:S(2)}) collective-permute-start(f32[1280,400]{0,1:T(8,128)} %pad_maximum_fusion.7), channel_id=1, source_target_pairs={{0,2},{1,3},{2,4},{3,5},{4,6},{5,7},{6,0},{7,1}} | collective-permute-start | bytes 6144008 | tf_op jit(solution)/shard_map/ppermute | solution.py:71
  251.9 10.5 copy-start.61
  251.9 75.0 %copy-start.39 = (f32[237]{0:T(256)S(1)}, f32[237]{0:T(256)}, u32[]{:S(2)}) copy-start(f32[237]{0:T(256)} %copy-done.38) | copy-start | bytes 2848
  251.9 75.1 %copy-start.25 = (f32[1024,200]{0,1:T(8,128)S(1)}, f32[1024,200]{0,1:T(8,128)}, u32[]{:S(2)}) copy-start(f32[1024,200]{0,1:T(8,128)} %get-tuple-element.100) | copy-start | bytes 2457604
  253.7 73.3 %copy-start.26 = (f32[1024,200]{0,1:T(8,128)S(1)}, f32[1024,200]{0,1:T(8,128)}, u32[]{:S(2)}) copy-start(f32[1024,200]{0,1:T(8,128)} %get-tuple-element.101) | copy-start | bytes 2457604
  262.3 232.8 %all-reduce.11.cloned.1.call-start = ((), (), s32[]{:S(2)}) async-start(), calls=%async_computation.2 | async-start | bytes 983040 | tf_op jit(solution)/shard_map/psum | solution.py:73
  395.7 31.7 %collective-permute-start.7 = (bf16[1280,400]{0,1:T(8,128)(2,1)}, bf16[1280,400]{0,1:T(8,128)(2,1)}, u32[]{:S(2)}, u32[]{:S(2)}) collective-permute-start(bf16[1280,400]{0,1:T(8,128)(2,1)} %copy.72), channel_id=1, source_target_pairs={{3,0},{4,1},{5,2},{6,3},{7,4},{0,5},{1,6},{2,7}} | collective-permute-start | bytes 3072008 | tf_op jit(solution)/shard_map/ppermute | solution.py:69
  433.2 63.0 %collective-permute-start.8 = (f32[1280,400]{0,1:T(8,128)}, f32[1280,400]{0,1:T(8,128)}, u32[]{:S(2)}, u32[]{:S(2)}) collective-permute-start(f32[1280,400]{0,1:T(8,128)} %pad_maximum_fusion.8), channel_id=1, source_target_pairs={{0,3},{1,4},{2,5},{3,6},{4,7},{5,0},{6,1},{7,2}} | collective-permute-start | bytes 6144008 | tf_op jit(solution)/shard_map/ppermute | solution.py:71
  437.9 10.4 copy-start.60
  437.9 58.3 %copy-start.40 = (f32[237]{0:T(256)S(1)}, f32[237]{0:T(256)}, u32[]{:S(2)}) copy-start(f32[237]{0:T(256)} %copy-done.38) | copy-start | bytes 2848
  437.9 58.3 %copy-start.27 = (f32[1024,200]{0,1:T(8,128)S(1)}, f32[1024,200]{0,1:T(8,128)}, u32[]{:S(2)}) copy-start(f32[1024,200]{0,1:T(8,128)} %get-tuple-element.98) | copy-start | bytes 2457604
  439.7 56.5 %copy-start.28 = (f32[1024,200]{0,1:T(8,128)S(1)}, f32[1024,200]{0,1:T(8,128)}, u32[]{:S(2)}) copy-start(f32[1024,200]{0,1:T(8,128)} %get-tuple-element.99) | copy-start | bytes 2457604
  447.9 208.9 %all-reduce.13.cloned.1.call-start = ((), (), s32[]{:S(2)}) async-start(), calls=%async_computation.3 | async-start | bytes 983040 | tf_op jit(solution)/shard_map/psum | solution.py:73
  564.8 25.5 %collective-permute-start.10 = (bf16[1280,400]{0,1:T(8,128)(2,1)}, bf16[1280,400]{0,1:T(8,128)(2,1)}, u32[]{:S(2)}, u32[]{:S(2)}) collective-permute-start(bf16[1280,400]{0,1:T(8,128)(2,1)} %copy.79), channel_id=1, source_target_pairs={{4,0},{5,1},{6,2},{7,3},{0,4},{1,5},{2,6},{3,7}} | collective-permute-start | bytes 3072008 | tf_op jit(solution)/shard_map/ppermute | solution.py:69
  596.2 61.7 %collective-permute-start.11 = (f32[1280,400]{0,1:T(8,128)}, f32[1280,400]{0,1:T(8,128)}, u32[]{:S(2)}, u32[]{:S(2)}) collective-permute-start(f32[1280,400]{0,1:T(8,128)} %pad_maximum_fusion.9), channel_id=1, source_target_pairs={{0,4},{1,5},{2,6},{3,7},{4,0},{5,1},{6,2},{7,3}} | collective-permute-start | bytes 6144008 | tf_op jit(solution)/shard_map/ppermute | solution.py:71
  602.0 10.2 copy-start.59
  602.0 56.0 %copy-start.19 = (f32[1024,200]{0,1:T(8,128)S(1)}, f32[1024,200]{0,1:T(8,128)}, u32[]{:S(2)}) copy-start(f32[1024,200]{0,1:T(8,128)} %get-tuple-element.96) | copy-start | bytes 2457604
  603.8 54.2 %copy-start.20 = (f32[1024,200]{0,1:T(8,128)S(1)}, f32[1024,200]{0,1:T(8,128)}, u32[]{:S(2)}) copy-start(f32[1024,200]{0,1:T(8,128)} %get-tuple-element.97) | copy-start | bytes 2457604
  612.1 211.2 %all-reduce.15.cloned.1.call-start = ((), (), s32[]{:S(2)}) async-start(), calls=%async_computation.4 | async-start | bytes 983040 | tf_op jit(solution)/shard_map/psum | solution.py:73
  726.9 28.1 %collective-permute-start.13 = (bf16[1280,400]{0,1:T(8,128)(2,1)}, bf16[1280,400]{0,1:T(8,128)(2,1)}, u32[]{:S(2)}, u32[]{:S(2)}) collective-permute-start(bf16[1280,400]{0,1:T(8,128)(2,1)} %copy.86), channel_id=1, source_target_pairs={{5,0},{6,1},{7,2},{0,3},{1,4},{2,5},{3,6},{4,7}} | collective-permute-start | bytes 3072008 | tf_op jit(solution)/shard_map/ppermute | solution.py:69
  749.4 4.1 copy-start.3
  760.9 63.5 %collective-permute-start.14 = (f32[1280,400]{0,1:T(8,128)}, f32[1280,400]{0,1:T(8,128)}, u32[]{:S(2)}, u32[]{:S(2)}) collective-permute-start(f32[1280,400]{0,1:T(8,128)} %pad_maximum_fusion.10), channel_id=1, source_target_pairs={{0,5},{1,6},{2,7},{3,0},{4,1},{5,2},{6,3},{7,4}} | collective-permute-start | bytes 6144008 | tf_op jit(solution)/shard_map/ppermute | solution.py:71
  766.2 10.2 copy-start.58
  766.2 58.3 %copy-start.21 = (f32[1024,200]{0,1:T(8,128)S(1)}, f32[1024,200]{0,1:T(8,128)}, u32[]{:S(2)}) copy-start(f32[1024,200]{0,1:T(8,128)} %get-tuple-element.94) | copy-start | bytes 2457604
  768.0 56.5 %copy-start.22 = (f32[1024,200]{0,1:T(8,128)S(1)}, f32[1024,200]{0,1:T(8,128)}, u32[]{:S(2)}) copy-start(f32[1024,200]{0,1:T(8,128)} %get-tuple-element.95) | copy-start | bytes 2457604
  776.3 231.1 %all-reduce.17.cloned.1.call-start = ((), (), s32[]{:S(2)}) async-start(), calls=%async_computation.5 | async-start | bytes 983040 | tf_op jit(solution)/shard_map/psum | solution.py:73
  893.0 25.5 %collective-permute-start.16 = (bf16[1280,400]{0,1:T(8,128)(2,1)}, bf16[1280,400]{0,1:T(8,128)(2,1)}, u32[]{:S(2)}, u32[]{:S(2)}) collective-permute-start(bf16[1280,400]{0,1:T(8,128)(2,1)} %copy.93), channel_id=1, source_target_pairs={{6,0},{7,1},{0,2},{1,3},{2,4},{3,5},{4,6},{5,7}} | collective-permute-start | bytes 3072008 | tf_op jit(solution)/shard_map/ppermute | solution.py:69
  924.4 86.2 %collective-permute-start.17 = (f32[1280,400]{0,1:T(8,128)}, f32[1280,400]{0,1:T(8,128)}, u32[]{:S(2)}, u32[]{:S(2)}) collective-permute-start(f32[1280,400]{0,1:T(8,128)} %pad_maximum_fusion.11), channel_id=1, source_target_pairs={{0,6},{1,7},{2,0},{3,1},{4,2},{5,3},{6,4},{7,5}} | collective-permute-start | bytes 6144008 | tf_op jit(solution)/shard_map/ppermute | solution.py:71
  930.3 10.2 copy-start.57
  932.1 78.5 %copy-start.17 = (f32[1024,200]{0,1:T(8,128)S(1)}, f32[1024,200]{0,1:T(8,128)}, u32[]{:S(2)}) copy-start(f32[1024,200]{0,1:T(8,128)} %get-tuple-element.92) | copy-start | bytes 2457604
  932.1 78.5 %copy-start.18 = (f32[1024,200]{0,1:T(8,128)S(1)}, f32[1024,200]{0,1:T(8,128)}, u32[]{:S(2)}) copy-start(f32[1024,200]{0,1:T(8,128)} %get-tuple-element.93) | copy-start | bytes 2457604
  (38 other events, 97.3 us)
Sparse Core Ops, SparseCore 0:
  100.8 42.6 all-reduce.6
  262.4 63.3 all-reduce.8
  448.0 47.0 all-reduce.10
  612.2 44.5 all-reduce.12
  776.4 46.8 all-reduce.14
  940.6 66.7 all-reduce.16
where the time goes:
time: 1110 us; the launch traced here: 1090 us
  other arithmetic  425 us (38%)
  waiting for transfers between devices  308 us (28%)
  local copies, waits for them, and re-layouts  298 us (27%)
  matrix products  21.5 us (2%)
  starting transfers between devices  19.9 us (2%)
  between operations  19.9 us (2%)
    psum x6, waiting for transfers between devices, per_device(): lax.psum(jax.ops.segment_sum(d_rel, rel_ids, num_segments=rel_count), 'ent')  305 us
    scatter-add x6, other arithmetic, per_device(): jax.ops.segment_sum(jnp.concatenate([d_head, returned]), jnp.concatenate(...  138 us
    sub x12, other arithmetic, adagrad_rows(): table - LEARN_RATE * row_grad / jnp.sqrt(new_state + ADA_EPS)[:, None]  109 us
    unnamed x152, local copies, waits for them, and re-layouts  74.8 us
    gather x12, local copies, waits for them, and re-layouts, per_device(): ent_part[served].astype(jnp.bfloat16)  69.7 us
    gather x6, local copies, waits for them, and re-layouts, per_device(): ent_part[head_ids]  60 us
    scatter-add x6, other arithmetic, per_device(): jax.ops.segment_sum(d_rel, rel_ids, num_segments=rel_count)  49.5 us
    reduce_sum x12, other arithmetic, adagrad_rows(): new_state = state + jnp.mean(row_grad * row_grad, axis=1)  49.4 us
  transfers between devices with their start and end apart: 24, of which 7 were waited for; matrix products, arithmetic and copies ran while one was open for 54% of the time, Pallas kernels for 0%

commit v1 on v0

v1 whole, which is shorter than its diff:
```python
import functools

import jax
import jax.numpy as jnp
from jax import lax
from jax.experimental import pallas as pl
from jax.experimental.pallas import tpu as pltpu
from jax.sharding import PartitionSpec as P

LEARN_RATE = 0.25
ADA_EPS = 1e-10
LANES = 128
SUB = 32
CHUNK = 256
REL_ROWS = 256
VMEM = pltpu.VMEM
SMEM = pltpu.SMEM
F32 = jnp.float32
BF16 = jnp.bfloat16


def lane_iota(rows):
    return lax.broadcasted_iota(jnp.int32, (rows, LANES), 1)


def updated(e, a, emb_dim, lane):
    squares = (a[0] * a[0] + a[1] * a[1]) + (a[2] * a[2] + a[3] * a[3])
    state = jnp.sum(squares * (1.0 / emb_dim) + jnp.where(lane == LANES - 1, e[1], 0.0), axis=1, keepdims=True)
    scale = LEARN_RATE * lax.rsqrt(state + ADA_EPS)
    new = [e[c] - scale * a[c] for c in range(4)]
    new[1] = jnp.where(lane == LANES - 1, state, new[1])
    return new


def split3(x):
    hi = x.astype(BF16)
    rest = x - hi.astype(F32)
    mid = rest.astype(BF16)
    return hi, mid, (rest - mid.astype(F32)).astype(BF16)


def write_wire(buf, n, b, x, short, left, lane):
    base = b * SUB
    turned = pltpu.roll(x[3], short, axis=1)
    over = 2 * short - LANES
    rows = lambda part: pl.ds(pl.multiple_of(part * CHUNK + base, SUB), SUB)
    buf[n, rows(0), :] = x[0].astype(BF16)
    buf[n, rows(1), :] = x[2].astype(BF16)
    buf[n, rows(2), :] = jnp.where(lane < short, x[1], turned).astype(BF16)
    return left + pltpu.roll(jnp.where(lane < over, turned, 0.0), b * over, axis=1)


def read_wire(buf, n, b, short, left, lane):
    base = b * SUB
    rows = lambda part: pl.ds(pl.multiple_of(part * CHUNK + base, SUB), SUB)
    over = 2 * short - LANES
    x0 = buf[n, rows(0), :].astype(F32)
    x2 = buf[n, rows(1), :].astype(F32)
    mixed = buf[n, rows(2), :].astype(F32)
    x1 = jnp.where(lane < short, mixed, 0.0)
    kept = LANES - short
    tail = pltpu.roll(left, lax.rem(LANES + kept - b * over, LANES), axis=1)
    x3 = jnp.where(lane < kept, pltpu.roll(mixed, kept, axis=1), jnp.where(lane < short, tail, 0.0))
    return [x0, x1, x2, x3]


def load4(ref, at):
    return [ref[pl.ds(at, SUB), c, :] for c in range(4)]


def gather_rows(ref, acc, idx, start, rows_e, rows_a):
    for i in range(SUB):
        r = idx[start + i]
        rows_e[i] = ref[r]
        rows_a[i] = acc[r]


def dense_update(ent, acc, first, count, emb_dim):
    lane = lane_iota(SUB)
    zero = jnp.zeros((SUB, LANES), F32)

    def step(j, carry):
        at = pl.multiple_of((first + j) * SUB, SUB)
        new = updated(load4(ent, at), load4(acc, at), emb_dim, lane)
        for c in range(4):
            ent[pl.ds(at, SUB), c, :] = new[c]
            acc[pl.ds(at, SUB), c, :] = zero
        return carry

    lax.fori_loop(0, count, step, 0)


def main_kernel(shift, devs, emb_dim, head_idx, serve_idx, rel_idx, weight, rel_in, ent_in, acc_in,
                ent, acc, grads, rel_out, loss_out,
                rows_e, rows_a, rel_split, heads, rels, served, q_send, q_recv, dq_send, dq_recv, q_all, weights, scores,
                pos, d_pos, probs, d_neg, d_mix, d_split, rel_acc, rel_got, rel_half, rel_got1, rel_two, rel_got2, rel_sum,
                loss_send, loss_recv, q_ss, q_rs, d_ss, d_rs, r_ss, r_rs):
    edges = head_idx.shape[0]
    negs = serve_idx.shape[0] - edges
    chunks = edges // CHUNK
    subs = CHUNK // SUB
    half = emb_dim // 2
    short = half - LANES
    score_scale = emb_dim ** -0.5
    me = lax.axis_index("ent")
    owner = lax.rem(me + shift, devs)
    asker = lax.rem(me + devs - shift, devs)
    core = lax.rem(me, 2)
    x_at = lax.rem(me // 2, 2)
    y_at = me // 4
    mate = me + 1 - 2 * core
    x_mate = me + 2 - 4 * x_at
    y_mate = me + 4 - 8 * y_at
    lane = lane_iota(SUB)

    def copy_to(src, dst, send_sem, recv_sem, dev):
        return pltpu.make_async_remote_copy(src_ref=src, dst_ref=dst, send_sem=send_sem, recv_sem=recv_sem,
                                            device_id={"ent": dev}, device_id_type=pl.DeviceIdType.MESH)

    barrier = pltpu.get_barrier_semaphore()
    for dev in (owner, asker, mate, x_mate, y_mate):
        pl.semaphore_signal(barrier, inc=1, device_id={"ent": dev}, device_id_type=pl.DeviceIdType.MESH)

    def split_rel(j, carry):
        at = pl.ds(pl.multiple_of(j * SUB, SUB), SUB)
        for p, part in enumerate(split3(rel_in[at, :])):
            rel_split[at, 512 * p:512 * (p + 1)] = part
        return carry

    lax.fori_loop(0, REL_ROWS // SUB, split_rel, 0)

    def one_hot(n):
        ids = rel_idx[n:n + 1, :]
        return jnp.where(lax.broadcasted_iota(jnp.int32, (REL_ROWS, CHUNK), 0) == ids, 1.0, 0.0).astype(BF16)

    q_copies = []
    for n in range(chunks):
        picked = lax.dot_general(one_hot(n), rel_split[...], (((0,), (0,)), ((), ())), preferred_element_type=F32)
        rels[n * CHUNK:(n + 1) * CHUNK, :] = (picked[:, :512] + picked[:, 512:1024]) + picked[:, 1024:]

        def query(b, left, n=n):
            at = pl.multiple_of(n * CHUNK + b * SUB, SUB)
            gather_rows(ent_in, acc_in, head_idx, at, rows_e, rows_a)
            h = updated(load4(rows_e, 0), load4(rows_a, 0), emb_dim, lane)
            h[1] = jnp.where(lane < short, h[1], 0.0)
            r = [rels[pl.ds(at, SUB), LANES * c:LANES * (c + 1)] for c in range(4)]
            r[1] = jnp.where(lane < short, r[1], 0.0)
            for c in range(4):
                heads[pl.ds(at, SUB), LANES * c:LANES * (c + 1)] = h[c]
            q = [h[0] * r[0] - h[2] * r[2], h[1] * r[1] - h[3] * r[3], h[0] * r[2] + h[2] * r[0], h[1] * r[3] + h[3] * r[1]]
            return write_wire(q_send, n, b, q, short, left, lane)

        left = lax.fori_loop(0, subs, query, jnp.zeros((SUB, LANES), F32))
        q_send[n, 3 * CHUNK:, :] = left.astype(BF16)
        if n == 0:
            pl.semaphore_wait(barrier, 5)
        copy = copy_to(q_send.at[n], q_recv.at[n], q_ss.at[n], q_rs.at[n], owner)
        copy.start()
        q_copies.append(copy)

    def serve(j, carry):
        at = pl.multiple_of(j * SUB, SUB)
        gather_rows(ent_in, acc_in, serve_idx, at, rows_e, rows_a)
        t = updated(load4(rows_e, 0), load4(rows_a, 0), emb_dim, lane)
        t[1] = jnp.where(lane < short, t[1], 0.0)
        for c in range(4):
            served[pl.ds(at, SUB), LANES * c:LANES * (c + 1)] = t[c].astype(BF16)
        return carry

    lax.fori_loop(0, (edges + negs) // SUB, serve, 0)

    steps = ent.shape[0] // SUB
    loss = jnp.zeros((SUB, 1), F32)
    d_copies = []
    for n in range(chunks):
        dense_update(ent, acc, n * (steps // chunks), steps // chunks, emb_dim)
        for p in range(CHUNK // LANES):
            row = jnp.broadcast_to(weight[n:n + 1, LANES * p:LANES * (p + 1)], (LANES, LANES))
            weights[LANES * p:LANES * (p + 1), :] = jnp.transpose(row)
        copy_to(q_send.at[n], q_recv.at[n], q_ss.at[n], q_rs.at[n], owner).wait_recv()

        def arrive(b, carry, n=n):
            at = pl.multiple_of(b * SUB, SUB)
            q = read_wire(q_recv, n, b, short, q_recv[n, 3 * CHUNK:, :].astype(F32), lane)
            t = [served[pl.ds(pl.multiple_of(n * CHUNK + at, SUB), SUB), LANES * c:LANES * (c + 1)].astype(F32) for c in range(4)]
            pos[pl.ds(at, SUB), :] = score_scale * jnp.sum((q[0] * t[0] + q[1] * t[1]) + (q[2] * t[2] + q[3] * t[3]), axis=1, keepdims=True)
            for c in range(4):
                q_all[pl.ds(at, SUB), LANES * c:LANES * (c + 1)] = q[c].astype(BF16)
            return carry

        lax.fori_loop(0, subs, arrive, 0)
        scores[...] = lax.dot_general(q_all[...], served[edges:, :], (((1,), (1,)), ((), ())), preferred_element_type=F32)

        def soft(b, total):
            at = pl.ds(pl.multiple_of(b * SUB, SUB), SUB)
            s = score_scale * scores[at, :]
            p = pos[at, :]
            w = weights[at, 0:1]
            top = jnp.maximum(p, jnp.max(s, axis=1, keepdims=True))
            e = jnp.exp(s - top)
            pe = jnp.exp(p - top)
            denom = pe + jnp.sum(e, axis=1, keepdims=True)
            d_pos[at, :] = score_scale * (w * (pe / denom - 1.0))
            probs[at, :] = ((w / denom) * e).astype(BF16)
            return total + w * (top + jnp.log(denom) - p)

        loss = lax.fori_loop(0, subs, soft, loss)
        d_mix[...] = jnp.dot(probs[...], served[edges:, :], preferred_element_type=F32)
        part = lax.dot_general(probs[...], q_all[...], (((0,), (0,)), ((), ())), preferred_element_type=F32)
        if n == 0:
            d_neg[...] = part
        else:
            d_neg[...] += part

        def back(b, left, n=n):
            at = pl.multiple_of(b * SUB, SUB)
            dp = d_pos[pl.ds(at, SUB), :]
            dq = []
            for c in range(4):
                cols = slice(LANES * c, LANES * (c + 1))
                t = served[pl.ds(pl.multiple_of(n * CHUNK + at, SUB), SUB), cols].astype(F32)
                q = q_all[pl.ds(at, SUB), cols].astype(F32)
                dq.append(dp * t + score_scale * d_mix[pl.ds(at, SUB), cols])
                grads[pl.ds(pl.multiple_of(edges + n * CHUNK + at, SUB), SUB), c, :] = dp * q
            return write_wire(dq_send, n, b, dq, short, left, lane)

        left = lax.fori_loop(0, subs, back, jnp.zeros((SUB, LANES), F32))
        dq_send[n, 3 * CHUNK:, :] = left.astype(BF16)
        copy = copy_to(dq_send.at[n], dq_recv.at[n], d_ss.at[n], d_rs.at[n], asker)
        copy.start()
        d_copies.append(copy)

    loss_send[...] = jnp.broadcast_to(jnp.sum(loss, axis=0, keepdims=True), (8, LANES))
    loss_copy = copy_to(loss_send, loss_recv, r_ss.at[6], r_rs.at[6], asker)
    loss_copy.start()

    def neg_rows(b, carry):
        at = pl.multiple_of(b * SUB, SUB)
        for c in range(4):
            grads[pl.ds(pl.multiple_of(2 * edges + at, SUB), SUB), c, :] = score_scale * d_neg[pl.ds(at, SUB), LANES * c:LANES * (c + 1)]
        return carry

    lax.fori_loop(0, negs // SUB, neg_rows, 0)

    for n in range(chunks):
        copy_to(dq_send.at[n], dq_recv.at[n], d_ss.at[n], d_rs.at[n], asker).wait_recv()

        def own(b, carry, n=n):
            at = pl.multiple_of(n * CHUNK + b * SUB, SUB)
            dq = read_wire(dq_recv, n, b, short, dq_recv[n, 3 * CHUNK:, :].astype(F32), lane)
            h = [heads[pl.ds(at, SUB), LANES * c:LANES * (c + 1)] for c in range(4)]
            r = [rels[pl.ds(at, SUB), LANES * c:LANES * (c + 1)] for c in range(4)]
            r[1] = jnp.where(lane < short, r[1], 0.0)
            dh = [dq[0] * r[0] + dq[2] * r[2], dq[1] * r[1] + dq[3] * r[3], dq[2] * r[0] - dq[0] * r[2], dq[3] * r[1] - dq[1] * r[3]]
            dr = [dq[0] * h[0] + dq[2] * h[2], dq[1] * h[1] + dq[3] * h[3], dq[2] * h[0] - dq[0] * h[2], dq[3] * h[1] - dq[1] * h[3]]
            row = pl.ds(pl.multiple_of(b * SUB, SUB), SUB)
            for c in range(4):
                grads[pl.ds(at, SUB), c, :] = dh[c]
                for p, part in enumerate(split3(dr[c])):
                    d_split[row, 512 * p + LANES * c:512 * p + LANES * (c + 1)] = part
            return carry

        lax.fori_loop(0, subs, own, 0)
        part = jnp.dot(one_hot(n), d_split[...], preferred_element_type=F32)
        part = (part[:, :512] + part[:, 512:1024]) + part[:, 1024:]
        if n == 0:
            rel_acc[...] = part
        else:
            rel_acc[...] += part

    hrows = REL_ROWS // 2
    qrows = hrows // 2
    mine = pl.ds(pl.multiple_of(core * hrows, hrows), hrows)
    theirs = pl.ds(pl.multiple_of((1 - core) * hrows, hrows), hrows)
    c0 = copy_to(rel_acc.at[theirs], rel_got, r_ss.at[0], r_rs.at[0], mate)
    c0.start()
    c0.wait_recv()
    rel_half[...] = (rel_acc[mine, :] + rel_got[...]).astype(BF16)
    first, last = pl.ds(0, qrows), pl.ds(qrows, qrows)
    c1 = copy_to(rel_half.at[first], rel_got1.at[first], r_ss.at[1], r_rs.at[1], x_mate)
    c2 = copy_to(rel_half.at[last], rel_got1.at[last], r_ss.at[2], r_rs.at[2], y_mate)
    c1.start()
    c2.start()
    c1.wait_recv()
    rel_two[first, :] = (rel_half[first, :].astype(F32) + rel_got1[first, :].astype(F32)).astype(BF16)
    c3 = copy_to(rel_two.at[first], rel_got2.at[first], r_ss.at[3], r_rs.at[3], y_mate)
    c3.start()
    c2.wait_recv()
    rel_two[last, :] = (rel_half[last, :].astype(F32) + rel_got1[last, :].astype(F32)).astype(BF16)
    c4 = copy_to(rel_two.at[last], rel_got2.at[last], r_ss.at[4], r_rs.at[4], x_mate)
    c4.start()
    c3.wait_recv()
    c4.wait_recv()
    rel_sum[mine, :] = rel_two[...].astype(F32) + rel_got2[...].astype(F32)
    c5 = copy_to(rel_sum.at[mine], rel_sum.at[mine], r_ss.at[5], r_rs.at[5], mate)
    c5.start()
    c5.wait_recv()

    def rel_step(j, carry):
        at = pl.ds(pl.multiple_of(j * SUB, SUB), SUB)
        cols = [slice(LANES * c, LANES * (c + 1)) for c in range(4)]
        new = updated([rel_in[at, s] for s in cols], [rel_sum[at, s] for s in cols], emb_dim, lane)
        for c in range(4):
            rel_out[at, cols[c]] = new[c]
        return carry

    lax.fori_loop(0, REL_ROWS // SUB, rel_step, 0)
    loss_copy.wait_recv()
    loss_out[...] = loss_recv[...]
    for copy in q_copies + d_copies + [loss_copy, c0, c1, c2, c3, c4, c5]:
        copy.wait_send()


def scatter_kernel(idx, flags, grads, acc_in, acc):
    group = idx.shape[0] // flags.shape[0]

    def step(j, carry):
        at = j * group
        rows = [idx[at + i] for i in range(group)]

        @pl.when(flags[j] == 0)
        def _():
            new = [acc[rows[i]] + grads[at + i] for i in range(group)]
            for i in range(group):
                acc[rows[i]] = new[i]

        @pl.when(flags[j] != 0)
        def _():
            for i in range(group):
                acc[rows[i]] = acc[rows[i]] + grads[at + i]

        return carry

    lax.fori_loop(0, flags.shape[0], step, 0)


def enter_kernel(table, state, ent, acc, pad):
    blk = pl.program_id(0)
    cols = table.shape[1]
    half = table.shape[0] // 2
    short = half - LANES
    for j in range(cols // LANES):
        at = pl.ds(pl.multiple_of(blk * cols + j * LANES, LANES), LANES)
        lanes = slice(LANES * j, LANES * (j + 1))
        rows = lax.broadcasted_iota(jnp.int32, (LANES - short, LANES), 0)
        for c in range(4):
            first = (c // 2) * half
            if c % 2 == 0:
                piece = table[first:first + LANES, lanes]
            else:
                pad[0:short, :] = table[first + LANES:first + half, lanes]
                if c == 1:
                    pad[short:, :] = jnp.where(rows == LANES - short - 1, state[j:j + 1, :], 0.0)
                else:
                    pad[short:, :] = jnp.zeros((LANES - short, LANES), F32)
                piece = pad[...]
            ent[at, c, :] = jnp.transpose(piece)
            acc[at, c, :] = jnp.zeros((LANES, LANES), F32)


def leave_kernel(emb_dim, ent, acc, table, state):
    blk = pl.program_id(0)
    cols = table.shape[1]
    half = emb_dim // 2
    short = half - LANES
    lane = lane_iota(LANES)
    for j in range(cols // LANES):
        at = pl.ds(pl.multiple_of(blk * cols + j * LANES, LANES), LANES)
        lanes = slice(LANES * j, LANES * (j + 1))
        new = updated([ent[at, c, :] for c in range(4)], [acc[at, c, :] for c in range(4)], emb_dim, lane)
        for c in range(4):
            first = (c // 2) * half
            turned = jnp.transpose(new[c])
            if c % 2 == 0:
                table[first:first + LANES, lanes] = turned
            else:
                table[first + LANES:first + half, lanes] = turned[0:short, :]
                if c == 1:
                    state[j:j + 1, :] = turned[LANES - 1:LANES, :]


def solution(mesh):
    devs = mesh.shape["ent"]
    row_spec = P(("sweep", "ent"), None)
    state_spec = P(("sweep", "ent"))
    rel_spec = P("sweep", None)
    edge_spec = P(("sweep", "ent"), None, None)
    in_vmem = pl.BlockSpec(memory_space=VMEM)
    in_smem = pl.BlockSpec(memory_space=SMEM)
    hold = lambda x: pltpu.with_memory_space_constraint(x, VMEM)

    def per_device(ent_part, ada_part, rel_table, head_idx, tail_idx, rel_idx, neg_idx, edge_mask):
        rows, emb_dim = ent_part.shape
        rounds, edges = head_idx.shape[1:]
        negs = neg_idx.shape[2]
        rel_count = rel_table.shape[0]
        half = emb_dim // 2
        chunks = edges // CHUNK
        total = 2 * edges + negs
        packed = jax.ShapeDtypeStruct((rows, 4, LANES), F32)
        table_vmem = VMEM(packed.shape, F32)
        block = 1024 if rows % 1024 == 0 else LANES * 8

        served, masks = [], []
        for step in range(rounds):
            pairs = [(s, (s + step + 1) % devs) for s in range(devs)]
            packet = jnp.concatenate([tail_idx[0, step], neg_idx[0, step], edge_mask[0, step]])
            got = lax.ppermute(packet, "ent", pairs)
            served.append(got[:edges + negs])
            masks.append(got[edges + negs:].astype(F32).reshape(chunks, CHUNK))
        all_idx = [jnp.concatenate([head_idx[0, s], served[s]]) for s in range(rounds)]
        group = 8
        grouped = jnp.stack(all_idx).reshape(rounds, total // group, group)
        same = (grouped[:, :, :, None] == grouped[:, :, None, :]) & jnp.triu(jnp.ones((group, group), bool), 1)
        flags = jnp.any(same, axis=(2, 3)).astype(jnp.int32)

        ent, acc = pl.pallas_call(
            enter_kernel,
            grid=(rows // block,),
            out_shape=(table_vmem, table_vmem),
            in_specs=[pl.BlockSpec((emb_dim, block), lambda i: (0, i)), pl.BlockSpec((block // LANES, LANES), lambda i: (i, 0))],
            out_specs=(in_vmem, in_vmem),
            scratch_shapes=[VMEM((LANES, LANES), F32)],
            compiler_params=pltpu.CompilerParams(vmem_limit_bytes=24 << 20),
            name="enter",
        )(ent_part.T, ada_part.reshape(rows // LANES, LANES))
        fill = 2 * LANES - half
        rel = jnp.pad(rel_table.reshape(rel_count, 2, half), ((0, REL_ROWS - rel_count), (0, 0), (0, fill))).reshape(REL_ROWS, 4 * LANES)

        wire = (chunks, 3 * CHUNK + SUB, LANES)
        full = (edges, 4 * LANES)
        losses = []
        for step in range(rounds):
            ent, acc, grads, rel, loss = pl.pallas_call(
                functools.partial(main_kernel, step + 1, devs, emb_dim),
                out_shape=(table_vmem, table_vmem, VMEM((total, 4, LANES), F32), VMEM((REL_ROWS, 4 * LANES), F32), jax.ShapeDtypeStruct((8, LANES), F32)),
                in_specs=[in_smem, in_smem] + [in_vmem] * 5,
                out_specs=(in_vmem,) * 5,
                input_output_aliases={5: 0, 6: 1},
                scratch_shapes=[
                    VMEM((SUB, 4, LANES), F32), VMEM((SUB, 4, LANES), F32), VMEM((REL_ROWS, 12 * LANES), BF16), VMEM(full, F32), VMEM(full, F32),
                    VMEM((edges + negs, 4 * LANES), BF16), VMEM(wire, BF16), VMEM(wire, BF16), VMEM(wire, BF16), VMEM(wire, BF16),
                    VMEM((CHUNK, 4 * LANES), BF16), VMEM((CHUNK, LANES), F32), VMEM((CHUNK, negs), F32),
                    VMEM((CHUNK, 1), F32), VMEM((CHUNK, 1), F32), VMEM((CHUNK, negs), BF16), VMEM((negs, 4 * LANES), F32), VMEM((CHUNK, 4 * LANES), F32),
                    VMEM((CHUNK, 12 * LANES), BF16), VMEM((REL_ROWS, 4 * LANES), F32), VMEM((REL_ROWS // 2, 4 * LANES), F32),
                    VMEM((REL_ROWS // 2, 4 * LANES), BF16), VMEM((REL_ROWS // 2, 4 * LANES), BF16), VMEM((REL_ROWS // 2, 4 * LANES), BF16), VMEM((REL_ROWS // 2, 4 * LANES), BF16),
                    VMEM((REL_ROWS, 4 * LANES), F32), VMEM((8, LANES), F32), VMEM((8, LANES), F32),
                ] + [pltpu.SemaphoreType.DMA((chunks,))] * 4 + [pltpu.SemaphoreType.DMA((7,))] * 2,
                compiler_params=pltpu.CompilerParams(collective_id=step, has_side_effects=True, vmem_limit_bytes=26 << 20),
                name="train",
            )(head_idx[0, step], served[step], rel_idx[0, step].reshape(chunks, CHUNK), masks[step], rel if step == 0 else hold(rel), hold(ent), hold(acc))
            acc = pl.pallas_call(
                scatter_kernel,
                out_shape=table_vmem,
                in_specs=[in_smem, in_smem, in_vmem, in_vmem],
                out_specs=in_vmem,
                input_output_aliases={3: 0},
                compiler_params=pltpu.CompilerParams(vmem_limit_bytes=4 << 20),
                name="scatter",
            )(all_idx[step], flags[step], hold(grads), hold(acc))
            losses.append(loss[0, 0] / edges)

        table_t, state = pl.pallas_call(
            functools.partial(leave_kernel, emb_dim),
            grid=(rows // block,),
            out_shape=(jax.ShapeDtypeStruct((emb_dim, rows), F32), jax.ShapeDtypeStruct((rows // LANES, LANES), F32)),
            in_specs=[in_vmem, in_vmem],
            out_specs=(pl.BlockSpec((emb_dim, block), lambda i: (0, i)), pl.BlockSpec((block // LANES, LANES), lambda i: (i, 0))),
            compiler_params=pltpu.CompilerParams(vmem_limit_bytes=24 << 20),
            name="leave",
        )(hold(ent), hold(acc))
        rel_final = rel.reshape(REL_ROWS, 2, 2 * LANES)[:rel_count, :, :half].reshape(rel_count, emb_dim)
        return table_t.T, state.reshape(rows), rel_final, jnp.stack(losses)[None, :]

    return jax.shard_map(per_device, mesh=mesh, in_specs=(row_spec, state_spec, rel_spec, edge_spec, edge_spec, edge_spec, edge_spec, edge_spec), out_specs=(row_spec, state_spec, rel_spec, row_spec), check_vma=False)
```

time: 1110 us -> 925 us (0.83)
  Pallas kernels: 0 us -> 806 us
  other arithmetic: 425 us -> 0.37 us
  waiting for transfers between devices: 308 us -> 2.23 us
  local copies, waits for them, and re-layouts: 298 us -> 92.5 us
  matrix products: 21.5 us -> 0 us
  between operations: 19.9 us -> 5.75 us
  starting transfers between devices: 19.9 us -> 8.24 us
    pallas_call x0 -> x14, Pallas kernels: none -> 806 us  [the longest x6 701 us: per_device(): pl.pallas_call(functools.partial(main_kernel, step + 1, devs, emb_dim), o...]
    psum x6 -> x0, waiting for transfers between devices: 305 us -> none  [per_device(): lax.psum(jax.ops.segment_sum(d_rel, rel_ids, num_segments=rel_count), 'ent')]
    scatter-add x12 -> x0, other arithmetic: 188 us -> none  [the longest x6 138 us: per_device(): jax.ops.segment_sum(jnp.concatenate([d_head, returned]), jnp.concatenate(...]
    gather x24 -> x0, local copies, waits for them, and re-layouts: 152 us -> none  [the longest x12 69.7 us: per_device(): ent_part[served].astype(jnp.bfloat16)]
    sub x18 -> x0, other arithmetic: 118 us -> none  [the longest x12 109 us: adagrad_rows(): table - LEARN_RATE * row_grad / jnp.sqrt(new_state + ADA_EPS)[:, None]]
    reduce_sum x30 -> x0, other arithmetic: 62.8 us -> none  [the longest x12 49.4 us: adagrad_rows(): new_state = state + jnp.mean(row_grad * row_grad, axis=1)]
    concatenate x12 -> x0, local copies, waits for them, and re-layouts: 44.1 us -> none  [the longest x6 33.4 us: per_device(): jnp.concatenate([d_head, returned])]
    concatenate x30 -> x12, other arithmetic: 36.2 us -> 0.07 us  [the longest x6 0.03 us: per_device(): jnp.concatenate([tail_idx[0, step], neg_idx[0, step], edge_mask[0, step]])]
  transfers between devices with their start and end apart: 24 -> 6, of which waited for: 7 -> 1; matrix products, arithmetic and copies ran while one was open for 54% -> 1% of each run, Pallas kernels for 0% -> 2%
where the time goes in v1:
time: 925 us; the launch traced here: 915 us
  Pallas kernels  806 us (87%)
  local copies, waits for them, and re-layouts  92.5 us (10%)
    pallas_call x6, Pallas kernels, per_device(): pl.pallas_call(functools.partial(main_kernel, step + 1, devs, emb_dim), o...  701 us
    unnamed x79, local copies, waits for them, and re-layouts  68.1 us
    pallas_call x6, Pallas kernels, per_device(): pl.pallas_call(scatter_kernel, out_shape=table_vmem, in_specs=[in_smem, i...  54.5 us
    pallas_call x1, Pallas kernels, per_device(): pl.pallas_call(functools.partial(leave_kernel, emb_dim), grid=(rows // bl...  30.7 us
    pallas_call x1, Pallas kernels, per_device(): pl.pallas_call(enter_kernel, grid=(rows // block,), out_shape=(table_vmem...  19.3 us
  transfers between devices with their start and end apart: 6, of which 1 were waited for; matrix products, arithmetic and copies ran while one was open for 1% of the time, Pallas kernels for 2%

profile of v1, /device:TPU:1, one launch (start us, length us, event | category | flops | bytes accessed | tf_op | source)
XLA Modules:
  0.0 915.0 jit_solution(16084193384202047384)
XLA Ops:
  0.6 0.8 fusion.2
  2.9 3.0 collective-permute-start
  6.0 1.1 collective-permute-start.1
  7.1 1.5 collective-permute-start.3
  8.6 1.4 collective-permute-start.5
  10.8 0.8 slice_reduce_fusion
  15.3 1.2 copy.52
  16.7 0.8 copy.66
  17.5 19.3 %enter.1 = (f32[8192,4,128]{2,1,0:T(4,128)S(1)}, f32[8192,4,128]{2,1,0:T(4,128)S(1)}) custom-call(f32[400,8192]{1,0:T(8,128)} %bitcast.41, f32[64,128]{1,0:T(8,128)} %bitcast.60), custom_call_target="tpu_custom_call" | custom-call | tf_op jit(solution)/shard_map/enter/pallas_call | solution.py:417
  36.9 5.7 copy-done
  42.6 5.7 copy-done.6
  48.3 1.2 collective-permute-start.4
  49.6 2.2 collective-permute-done.4
  58.8 5.8 copy-done.1
  64.6 5.8 copy-done.7
  70.3 115.8 %train.6 = (f32[8192,4,128]{2,1,0:T(4,128)S(1)}, f32[8192,4,128]{2,1,0:T(4,128)S(1)}, f32[2304,4,128]{2,1,0:T(4,128)S(1)}, f32[256,512]{1,0:T(8,128)S(1)}, f32[8,128]{1,0:T(8,128)}) custom-call(s32[1024]{0:T(1024)} %bitcast.59, s32[1280]{0:T(1024)} %copy-done.27, s32[4,256]{1,0:T(4,128)} %reshape_squeeze.23.rel_idx, ...), custom_call_target="tpu_custom_call", output_to_operand_aliasing={{0}: (5, {}), {1}: (6, {})} | custom-call | tf_op jit(solution)/shard_map/train/pallas_call | solution.py:434
  186.3 9.1 scatter.6.acc_in
  195.4 1.0 copy-done.13
  196.4 117.3 %train.7 = (f32[8192,4,128]{2,1,0:T(4,128)S(1)}, f32[8192,4,128]{2,1,0:T(4,128)S(1)}, f32[2304,4,128]{2,1,0:T(4,128)S(1)}, f32[256,512]{1,0:T(8,128)S(1)}, f32[8,128]{1,0:T(8,128)}) custom-call(s32[1024]{0:T(1024)} %bitcast.57, s32[1280]{0:T(1024)} %copy-done.26, s32[4,256]{1,0:T(4,128)} %reshape_squeeze.22.rel_idx, ...), custom_call_target="tpu_custom_call", output_to_operand_aliasing={{0}: (5, {}), {1}: (6, {})} | custom-call | tf_op jit(solution)/shard_map/train/pallas_call | solution.py:434
  313.7 9.1 scatter.7.acc_in
  322.9 1.0 copy-done.15
  323.9 116.8 %train.8 = (f32[8192,4,128]{2,1,0:T(4,128)S(1)}, f32[8192,4,128]{2,1,0:T(4,128)S(1)}, f32[2304,4,128]{2,1,0:T(4,128)S(1)}, f32[256,512]{1,0:T(8,128)S(1)}, f32[8,128]{1,0:T(8,128)}) custom-call(s32[1024]{0:T(1024)} %bitcast.55, s32[1280]{0:T(1024)} %copy-done.25, s32[4,256]{1,0:T(4,128)} %reshape_squeeze.21.rel_idx, ...), custom_call_target="tpu_custom_call", output_to_operand_aliasing={{0}: (5, {}), {1}: (6, {})} | custom-call | tf_op jit(solution)/shard_map/train/pallas_call | solution.py:434
  440.7 9.1 scatter.8.acc_in
  449.8 1.0 copy-done.17
  450.9 116.5 %train.9 = (f32[8192,4,128]{2,1,0:T(4,128)S(1)}, f32[8192,4,128]{2,1,0:T(4,128)S(1)}, f32[2304,4,128]{2,1,0:T(4,128)S(1)}, f32[256,512]{1,0:T(8,128)S(1)}, f32[8,128]{1,0:T(8,128)}) custom-call(s32[1024]{0:T(1024)} %bitcast.53, s32[1280]{0:T(1024)} %copy-done.24, s32[4,256]{1,0:T(4,128)} %reshape_squeeze.20.rel_idx, ...), custom_call_target="tpu_custom_call", output_to_operand_aliasing={{0}: (5, {}), {1}: (6, {})} | custom-call | tf_op jit(solution)/shard_map/train/pallas_call | solution.py:434
  567.4 9.1 scatter.9.acc_in
  576.5 1.0 copy-done.19
  577.6 116.7 %train.10 = (f32[8192,4,128]{2,1,0:T(4,128)S(1)}, f32[8192,4,128]{2,1,0:T(4,128)S(1)}, f32[2304,4,128]{2,1,0:T(4,128)S(1)}, f32[256,512]{1,0:T(8,128)S(1)}, f32[8,128]{1,0:T(8,128)}) custom-call(s32[1024]{0:T(1024)} %bitcast.51, s32[1280]{0:T(1024)} %copy-done.23, s32[4,256]{1,0:T(4,128)} %reshape_squeeze.19.rel_idx, ...), custom_call_target="tpu_custom_call", output_to_operand_aliasing={{0}: (5, {}), {1}: (6, {})} | custom-call | tf_op jit(solution)/shard_map/train/pallas_call | solution.py:434
  694.3 9.1 scatter.10.acc_in
  703.4 1.0 copy-done.21
  704.5 118.2 %train.11 = (f32[8192,4,128]{2,1,0:T(4,128)S(1)}, f32[8192,4,128]{2,1,0:T(4,128)S(1)}, f32[2304,4,128]{2,1,0:T(4,128)S(1)}, f32[256,512]{1,0:T(8,128)S(1)}, f32[8,128]{1,0:T(8,128)}) custom-call(s32[1024]{0:T(1024)} %bitcast.49, s32[1280]{0:T(1024)} %copy-done.22, s32[4,256]{1,0:T(4,128)} %reshape_squeeze.18.rel_idx, ...), custom_call_target="tpu_custom_call", output_to_operand_aliasing={{0}: (5, {}), {1}: (6, {})} | custom-call | tf_op jit(solution)/shard_map/train/pallas_call | solution.py:434
  822.7 5.7 copy-done.2
  828.4 5.7 copy-done.8
  834.1 2.2 copy-done.10
  836.8 1.0 copy.65
  837.8 1.2 slice.268
  839.0 1.2 slice.269
  841.5 1.2 slice.270
  843.3 1.2 slice.271
  845.1 1.2 slice.272
  847.0 1.2 slice.273
  848.8 5.8 copy-done.3
  854.6 2.3 copy-done.11
  856.9 9.1 scatter.11.acc
  866.0 5.7 copy-done.4
  871.8 5.8 copy-done.5
  877.5 5.8 copy-done.9
  883.3 30.7 %leave.1 = (f32[400,8192]{1,0:T(8,128)}, f32[64,128]{1,0:T(8,128)}) custom-call(f32[8192,4,128]{2,1,0:T(4,128)S(1)} %copy-done.9, f32[8192,4,128]{2,1,0:T(4,128)S(1)} %copy-done.5), custom_call_target="tpu_custom_call" | custom-call | tf_op jit(solution)/shard_map/leave/pallas_call | solution.py:463
  (140 shorter events, 14.0 us)
Async XLA Ops:
  2.9 50.2 %collective-permute-start = (s32[2304]{0:T(1024)S(1)}, s32[2304]{0:T(1024)S(1)}, u32[]{:S(2)}, u32[]{:S(2)}) collective-permute-start(s32[2304]{0:T(1024)S(1)} %pad_add_fusion), channel_id=1, source_target_pairs={{0,6},{1,7},{2,0},{3,1},{4,2},{5,3},{6,4},{7,5}} | collective-permute-start | bytes 27656 | tf_op jit(solution)/shard_map/ppermute | solution.py:408
  6.0 45.9 %collective-permute-start.1 = (s32[2304]{0:T(1024)S(1)}, s32[2304]{0:T(1024)S(1)}, u32[]{:S(2)}, u32[]{:S(2)}) collective-permute-start(s32[2304]{0:T(1024)S(1)} %pad_add_fusion.1), channel_id=1, source_target_pairs={{0,5},{1,6},{2,7},{3,0},{4,1},{5,2},{6,3},{7,4}} | collective-permute-start | bytes 27656 | tf_op jit(solution)/shard_map/ppermute | solution.py:408
  7.1 44.8 %collective-permute-start.2 = (s32[2304]{0:T(1024)S(1)}, s32[2304]{0:T(1024)S(1)}, u32[]{:S(2)}, u32[]{:S(2)}) collective-permute-start(s32[2304]{0:T(1024)S(1)} %pad_add_fusion.2), channel_id=1, source_target_pairs={{0,4},{1,5},{2,6},{3,7},{4,0},{5,1},{6,2},{7,3}} | collective-permute-start | bytes 27656 | tf_op jit(solution)/shard_map/ppermute | solution.py:408
  7.1 44.7 %collective-permute-start.3 = (s32[2304]{0:T(1024)S(1)}, s32[2304]{0:T(1024)S(1)}, u32[]{:S(2)}, u32[]{:S(2)}) collective-permute-start(s32[2304]{0:T(1024)S(1)} %pad_add_fusion.3), channel_id=1, source_target_pairs={{0,3},{1,4},{2,5},{3,6},{4,7},{5,0},{6,1},{7,2}} | collective-permute-start | bytes 27656 | tf_op jit(solution)/shard_map/ppermute | solution.py:408
  8.6 39.7 %collective-permute-start.5 = (s32[2304]{0:T(1024)S(1)}, s32[2304]{0:T(1024)S(1)}, u32[]{:S(2)}, u32[]{:S(2)}) collective-permute-start(s32[2304]{0:T(1024)S(1)} %pad_add_fusion.5), channel_id=1, source_target_pairs={{0,1},{1,2},{2,3},{3,4},{4,5},{5,6},{6,7},{7,0}} | collective-permute-start | bytes 27656 | tf_op jit(solution)/shard_map/ppermute | solution.py:408
  10.8 48.0 %copy-start.33 = (s32[1,1,1024]{2,0,1:T(1,128)}, s32[1,1,1024]{2,0,1:T(1,128)S(1)}, u32[]{:S(2)}) copy-start(s32[1,1,1024]{2,0,1:T(1,128)S(1)} %get-tuple-element.96) | copy-start | bytes 12292
  10.8 175.4 %copy-start.28 = (s32[1,1,1024]{2,0,1:T(1,128)}, s32[1,1,1024]{2,0,1:T(1,128)S(1)}, u32[]{:S(2)}) copy-start(s32[1,1,1024]{2,0,1:T(1,128)S(1)} %get-tuple-element.100) | copy-start | bytes 12292
  10.8 175.4 %copy-start.29 = (s32[1,1,1024]{2,0,1:T(1,128)}, s32[1,1,1024]{2,0,1:T(1,128)S(1)}, u32[]{:S(2)}) copy-start(s32[1,1,1024]{2,0,1:T(1,128)S(1)} %get-tuple-element.99) | copy-start | bytes 12292
  10.8 175.4 %copy-start.30 = (s32[1,1,1024]{2,0,1:T(1,128)}, s32[1,1,1024]{2,0,1:T(1,128)S(1)}, u32[]{:S(2)}) copy-start(s32[1,1,1024]{2,0,1:T(1,128)S(1)} %get-tuple-element.98) | copy-start | bytes 12292
  10.8 175.4 %copy-start.31 = (s32[1,1,1024]{2,0,1:T(1,128)}, s32[1,1,1024]{2,0,1:T(1,128)S(1)}, u32[]{:S(2)}) copy-start(s32[1,1,1024]{2,0,1:T(1,128)S(1)} %get-tuple-element.97) | copy-start | bytes 12292
  10.8 175.4 %copy-start.32 = (s32[1,1,1024]{2,0,1:T(1,128)}, s32[1,1,1024]{2,0,1:T(1,128)S(1)}, u32[]{:S(2)}) copy-start(s32[1,1,1024]{2,0,1:T(1,128)S(1)} %get-tuple-element.101) | copy-start | bytes 12292
  36.9 5.7 copy-start
  42.6 5.7 copy-start.6
  48.3 3.4 collective-permute-start.4
  49.5 9.2 %copy-start.27 = (s32[1280]{0:T(1024)}, s32[1280]{0:T(1024)S(1)}, u32[]{:S(2)}) copy-start(s32[1280]{0:T(1024)S(1)} %slice.284.serve_idx) | copy-start | bytes 15364
  51.8 134.5 %copy-start.26 = (s32[1280]{0:T(1024)}, s32[1280]{0:T(1024)S(1)}, u32[]{:S(2)}) copy-start(s32[1280]{0:T(1024)S(1)} %slice.282.serve_idx) | copy-start | bytes 15364
  51.8 134.4 %copy-start.25 = (s32[1280]{0:T(1024)}, s32[1280]{0:T(1024)S(1)}, u32[]{:S(2)}) copy-start(s32[1280]{0:T(1024)S(1)} %slice.280.serve_idx) | copy-start | bytes 15364
  51.9 134.4 %copy-start.24 = (s32[1280]{0:T(1024)}, s32[1280]{0:T(1024)S(1)}, u32[]{:S(2)}) copy-start(s32[1280]{0:T(1024)S(1)} %slice.278.serve_idx) | copy-start | bytes 15364
  51.9 134.4 %copy-start.23 = (s32[1280]{0:T(1024)}, s32[1280]{0:T(1024)S(1)}, u32[]{:S(2)}) copy-start(s32[1280]{0:T(1024)S(1)} %slice.276.serve_idx) | copy-start | bytes 15364
  53.2 133.1 %copy-start.22 = (s32[1280]{0:T(1024)}, s32[1280]{0:T(1024)S(1)}, u32[]{:S(2)}) copy-start(s32[1280]{0:T(1024)S(1)} %slice.274.serve_idx) | copy-start | bytes 15364
  58.8 5.8 copy-start.1
  64.6 5.8 copy-start.7
  186.3 9.1 copy-start.12
  195.4 1.0 copy-start.13
  313.7 9.1 copy-start.14
  322.8 1.0 copy-start.15
  440.7 9.1 copy-start.16
  449.8 1.0 copy-start.17
  567.4 9.1 copy-start.18
  576.5 1.0 copy-start.19
  694.3 9.1 copy-start.20
  703.4 1.0 copy-start.21
  822.7 5.7 copy-start.2
  828.4 5.7 copy-start.8
  834.1 2.2 copy-start.10
  848.8 5.8 copy-start.3
  854.6 2.3 copy-start.11
  866.0 5.7 copy-start.4
  871.8 5.8 copy-start.5
  877.5 5.8 copy-start.9

commit v2 on v1

v2 whole, which is shorter than its diff:
```python
import functools

import jax
import jax.numpy as jnp
from jax import lax
from jax.experimental import pallas as pl
from jax.experimental.pallas import tpu as pltpu
from jax.sharding import PartitionSpec as P

LEARN_RATE = 0.25
ADA_EPS = 1e-10
LANES = 128
SUB = 32
CHUNK = 256
REL_ROWS = 256
VMEM = pltpu.VMEM
SMEM = pltpu.SMEM
F32 = jnp.float32
BF16 = jnp.bfloat16


def lane_iota(rows):
    return lax.broadcasted_iota(jnp.int32, (rows, LANES), 1)


def updated(e, a, emb_dim, lane):
    squares = (a[0] * a[0] + a[1] * a[1]) + (a[2] * a[2] + a[3] * a[3])
    state = jnp.sum(squares * (1.0 / emb_dim) + jnp.where(lane == LANES - 1, e[1], 0.0), axis=1, keepdims=True)
    scale = LEARN_RATE * lax.rsqrt(state + ADA_EPS)
    new = [e[c] - scale * a[c] for c in range(4)]
    new[1] = jnp.where(lane == LANES - 1, state, new[1])
    return new


def split3(x):
    hi = x.astype(BF16)
    rest = x - hi.astype(F32)
    mid = rest.astype(BF16)
    return hi, mid, (rest - mid.astype(F32)).astype(BF16)


def write_wire(buf, n, b, x, short, left, lane):
    base = b * SUB
    turned = pltpu.roll(x[3], short, axis=1)
    over = 2 * short - LANES
    rows = lambda part: pl.ds(pl.multiple_of(part * CHUNK + base, SUB), SUB)
    buf[n, rows(0), :] = x[0].astype(BF16)
    buf[n, rows(1), :] = x[2].astype(BF16)
    buf[n, rows(2), :] = jnp.where(lane < short, x[1], turned).astype(BF16)
    return left + pltpu.roll(jnp.where(lane < over, turned, 0.0), b * over, axis=1)


def read_wire(buf, n, b, short, left, lane):
    base = b * SUB
    rows = lambda part: pl.ds(pl.multiple_of(part * CHUNK + base, SUB), SUB)
    over = 2 * short - LANES
    x0 = buf[n, rows(0), :].astype(F32)
    x2 = buf[n, rows(1), :].astype(F32)
    mixed = buf[n, rows(2), :].astype(F32)
    x1 = jnp.where(lane < short, mixed, 0.0)
    kept = LANES - short
    tail = pltpu.roll(left, lax.rem(LANES + kept - b * over, LANES), axis=1)
    x3 = jnp.where(lane < kept, pltpu.roll(mixed, kept, axis=1), jnp.where(lane < short, tail, 0.0))
    return [x0, x1, x2, x3]


def pieces(first, count):
    return [pl.ds(first * 4 + c, count, stride=4) for c in range(4)]


def row_of(r):
    return pl.ds(pl.multiple_of(r * 4, 4), 4)


def cols_of(c):
    return slice(LANES * c, LANES * (c + 1))


def gather_rows(ent, idx, step, start, rows):
    for i in range(SUB):
        r = idx[step, 0, start + i]
        rows[4 * i:4 * i + 4, :] = ent[r]
    return [rows[s, :] for s in pieces(0, SUB)]


def dense_update(ent, acc, first, count, emb_dim):
    lane = lane_iota(SUB)

    def step(j, carry):
        at = pl.multiple_of((first + j) * SUB, SUB)
        here = pieces(at, SUB)
        new = updated([ent[s, :] for s in here], [acc[s, :] for s in here], emb_dim, lane)
        for c in range(4):
            ent[here[c], :] = new[c]
        return carry

    lax.fori_loop(0, count, step, 0, unroll=2)


def merge_repeats(src, at, ids, split, grads, out):
    for p in range(LANES // SUB):
        part = pl.ds(pl.multiple_of(at + p * SUB, SUB), SUB)
        for c in range(4):
            for k, piece in enumerate(split3(src[part, cols_of(c)])):
                split[p * SUB:(p + 1) * SUB, 512 * k + LANES * c:512 * k + LANES * (c + 1)] = piece
    row = jnp.broadcast_to(ids, (LANES, LANES))
    i0 = lax.broadcasted_iota(jnp.int32, (LANES, LANES), 0)
    i1 = lane_iota(LANES)
    same = (jnp.transpose(row) == row) & (i1 <= i0) & (i1 // SUB == i0 // SUB)
    got = jnp.dot(jnp.where(same, 1.0, 0.0).astype(BF16), split[...], preferred_element_type=F32)
    here = pieces(out, LANES)
    for c in range(4):
        grads[here[c], :] = (got[:, cols_of(c)] + got[:, 512 + LANES * c:512 + LANES * (c + 1)]) + got[:, 1024 + LANES * c:1024 + LANES * (c + 1)]


def main_kernel(step, devs, emb_dim, head_idx, tail_idx, neg_idx, head_row, tail_row, neg_row, mask_row, rel_row, loss_in, rel_in, ent,
                grads, rel_out, loss_out,
                rows, rel_split, heads, rels, served, q_send, q_recv, dq_send, dq_recv, q_all, weights, scores,
                pos, d_pos, probs, d_mix, flat, d_head, d_split, m_split, rel_acc, rel_got, rel_half, rel_got1, rel_two, rel_got2, rel_sum,
                loss_send, loss_recv, q_ss, q_rs, d_ss, d_rs, r_ss, r_rs):
    edges = head_idx.shape[2]
    negs = neg_idx.shape[2]
    chunks = edges // CHUNK
    subs = CHUNK // SUB
    half = emb_dim // 2
    short = half - LANES
    score_scale = emb_dim ** -0.5
    shift = step + 1
    me = lax.axis_index("ent")
    owner = lax.rem(me + shift, devs)
    asker = lax.rem(me + devs - shift, devs)
    core = lax.rem(me, 2)
    x_at = lax.rem(me // 2, 2)
    y_at = me // 4
    mate = me + 1 - 2 * core
    x_mate = me + 2 - 4 * x_at
    y_mate = me + 4 - 8 * y_at
    lane = lane_iota(SUB)

    def copy_to(src, dst, send_sem, recv_sem, dev):
        return pltpu.make_async_remote_copy(src_ref=src, dst_ref=dst, send_sem=send_sem, recv_sem=recv_sem,
                                            device_id={"ent": dev}, device_id_type=pl.DeviceIdType.MESH)

    barrier = pltpu.get_barrier_semaphore()
    for dev in (owner, asker, mate, x_mate, y_mate):
        pl.semaphore_signal(barrier, inc=1, device_id={"ent": dev}, device_id_type=pl.DeviceIdType.MESH)
    def split_rel(j, carry):
        at = pl.ds(pl.multiple_of(j * SUB, SUB), SUB)
        for p, part in enumerate(split3(rel_in[at, :])):
            rel_split[at, 512 * p:512 * (p + 1)] = part
        return carry

    lax.fori_loop(0, REL_ROWS // SUB, split_rel, 0)
    def one_hot(n):
        ids = rel_row[step, 0:1, n * CHUNK:(n + 1) * CHUNK]
        return jnp.where(lax.broadcasted_iota(jnp.int32, (REL_ROWS, CHUNK), 0) == ids, 1.0, 0.0).astype(BF16)

    q_copies = []
    for n in range(chunks):
        picked = lax.dot_general(one_hot(n), rel_split[...], (((0,), (0,)), ((), ())), preferred_element_type=F32)
        rels[n * CHUNK:(n + 1) * CHUNK, :] = (picked[:, :512] + picked[:, 512:1024]) + picked[:, 1024:]

        def query(b, left, n=n):
            at = pl.multiple_of(n * CHUNK + b * SUB, SUB)
            h = gather_rows(ent, head_idx, step, at, rows)
            h[1] = jnp.where(lane < short, h[1], 0.0)
            r = [rels[pl.ds(at, SUB), cols_of(c)] for c in range(4)]
            r[1] = jnp.where(lane < short, r[1], 0.0)
            for c in range(4):
                heads[pl.ds(at, SUB), cols_of(c)] = h[c]
            q = [h[0] * r[0] - h[2] * r[2], h[1] * r[1] - h[3] * r[3], h[0] * r[2] + h[2] * r[0], h[1] * r[3] + h[3] * r[1]]
            return write_wire(q_send, n, b, q, short, left, lane)

        left = lax.fori_loop(0, subs, query, jnp.zeros((SUB, LANES), F32))
        q_send[n, 3 * CHUNK:, :] = left.astype(BF16)
        if n == 0:
            pl.semaphore_wait(barrier, 5)
        copy = copy_to(q_send.at[n], q_recv.at[n], q_ss.at[n], q_rs.at[n], owner)
        copy.start()
        q_copies.append(copy)

    def serve(idx, out):
        def one(j, carry):
            at = pl.multiple_of(j * SUB, SUB)
            t = gather_rows(ent, idx, step, at, rows)
            t[1] = jnp.where(lane < short, t[1], 0.0)
            for c in range(4):
                served[pl.ds(pl.multiple_of(out + at, SUB), SUB), cols_of(c)] = t[c].astype(BF16)
            return carry

        lax.fori_loop(0, idx.shape[2] // SUB, one, 0)

    serve(neg_idx, edges)
    serve(tail_idx, 0)

    loss = jnp.zeros((SUB, 1), F32)
    d_copies = []
    for n in range(chunks):
        for p in range(CHUNK // LANES):
            row = mask_row[step, 0:1, n * CHUNK + LANES * p:n * CHUNK + LANES * (p + 1)].astype(F32)
            weights[LANES * p:LANES * (p + 1), :] = jnp.transpose(jnp.broadcast_to(row, (LANES, LANES)))
        q_copies[n].wait_recv()

        def arrive(b, carry, n=n):
            at = pl.multiple_of(b * SUB, SUB)
            q = read_wire(q_recv, n, b, short, q_recv[n, 3 * CHUNK:, :].astype(F32), lane)
            t = [served[pl.ds(pl.multiple_of(n * CHUNK + at, SUB), SUB), cols_of(c)].astype(F32) for c in range(4)]
            pos[pl.ds(at, SUB), :] = score_scale * jnp.sum((q[0] * t[0] + q[1] * t[1]) + (q[2] * t[2] + q[3] * t[3]), axis=1, keepdims=True)
            for c in range(4):
                q_all[pl.ds(at, SUB), cols_of(c)] = q[c].astype(BF16)
            return carry

        lax.fori_loop(0, subs, arrive, 0)
        scores[...] = lax.dot_general(q_all[...], served[edges:, :], (((1,), (1,)), ((), ())), preferred_element_type=F32)

        def soft(b, total):
            at = pl.ds(pl.multiple_of(b * SUB, SUB), SUB)
            s = score_scale * scores[at, :]
            p = pos[at, :]
            w = weights[at, 0:1]
            top = jnp.maximum(p, jnp.max(s, axis=1, keepdims=True))
            e = jnp.exp(s - top)
            pe = jnp.exp(p - top)
            denom = pe + jnp.sum(e, axis=1, keepdims=True)
            d_pos[at, :] = score_scale * (w * (pe / denom - 1.0))
            probs[at, :] = ((w / denom) * e).astype(BF16)
            return total + w * (top + jnp.log(denom) - p)

        loss = lax.fori_loop(0, subs, soft, loss)
        d_mix[...] = jnp.dot(probs[...], served[edges:, :], preferred_element_type=F32)

        def back(b, left, n=n):
            at = pl.multiple_of(b * SUB, SUB)
            dp = d_pos[pl.ds(at, SUB), :]
            row = pl.ds(pl.multiple_of(n * CHUNK + at, SUB), SUB)
            dq = []
            for c in range(4):
                t = served[row, cols_of(c)].astype(F32)
                q = q_all[pl.ds(at, SUB), cols_of(c)].astype(F32)
                dq.append(dp * t + score_scale * d_mix[pl.ds(at, SUB), cols_of(c)])
                flat[row, cols_of(c)] = dp * q
            return write_wire(dq_send, n, b, dq, short, left, lane)

        left = lax.fori_loop(0, subs, back, jnp.zeros((SUB, LANES), F32))
        dq_send[n, 3 * CHUNK:, :] = left.astype(BF16)
        copy = copy_to(dq_send.at[n], dq_recv.at[n], d_ss.at[n], d_rs.at[n], asker)
        copy.start()
        d_copies.append(copy)
        part = lax.dot_general(probs[...], q_all[...], (((0,), (0,)), ((), ())), preferred_element_type=F32)
        if n == 0:
            flat[edges:, :] = part
        elif n < chunks - 1:
            flat[edges:, :] += part
        else:
            flat[edges:, :] = score_scale * (flat[edges:, :] + part)

    loss_send[...] = jnp.broadcast_to(jnp.sum(loss, axis=0, keepdims=True), (8, LANES))
    loss_copy = copy_to(loss_send, loss_recv, r_ss.at[6], r_rs.at[6], asker)
    loss_copy.start()

    def merge(ids, src_at, out):
        def one(j, carry):
            at = pl.multiple_of(j * LANES, LANES)
            merge_repeats(flat, src_at + at, ids[step, 0:1, pl.ds(at, LANES)], m_split, grads, out + at)
            return carry

        lax.fori_loop(0, ids.shape[2] // LANES, one, 0)

    merge(tail_row, 0, edges)
    merge(neg_row, edges, 2 * edges)

    for n in range(chunks):
        d_copies[n].wait_recv()

        def own(b, carry, n=n):
            at = pl.multiple_of(n * CHUNK + b * SUB, SUB)
            dq = read_wire(dq_recv, n, b, short, dq_recv[n, 3 * CHUNK:, :].astype(F32), lane)
            h = [heads[pl.ds(at, SUB), cols_of(c)] for c in range(4)]
            r = [rels[pl.ds(at, SUB), cols_of(c)] for c in range(4)]
            r[1] = jnp.where(lane < short, r[1], 0.0)
            dh = [dq[0] * r[0] + dq[2] * r[2], dq[1] * r[1] + dq[3] * r[3], dq[2] * r[0] - dq[0] * r[2], dq[3] * r[1] - dq[1] * r[3]]
            dr = [dq[0] * h[0] + dq[2] * h[2], dq[1] * h[1] + dq[3] * h[3], dq[2] * h[0] - dq[0] * h[2], dq[3] * h[1] - dq[1] * h[3]]
            row = pl.ds(pl.multiple_of(b * SUB, SUB), SUB)
            for c in range(4):
                d_head[row, cols_of(c)] = dh[c]
                for p, part in enumerate(split3(dr[c])):
                    d_split[row, 512 * p + LANES * c:512 * p + LANES * (c + 1)] = part
            return carry

        lax.fori_loop(0, subs, own, 0)
        part = jnp.dot(one_hot(n), d_split[...], preferred_element_type=F32)
        part = (part[:, :512] + part[:, 512:1024]) + part[:, 1024:]
        if n == 0:
            rel_acc[...] = part
        else:
            rel_acc[...] += part
        if n < chunks - 1:
            for p in range(CHUNK // LANES):
                at = n * CHUNK + p * LANES
                merge_repeats(d_head, p * LANES, head_row[step, 0:1, at:at + LANES], m_split, grads, at)

    hrows = REL_ROWS // 2
    qrows = hrows // 2
    mine = pl.ds(pl.multiple_of(core * hrows, hrows), hrows)
    theirs = pl.ds(pl.multiple_of((1 - core) * hrows, hrows), hrows)
    c0 = copy_to(rel_acc.at[theirs], rel_got, r_ss.at[0], r_rs.at[0], mate)
    c0.start()
    at = (chunks - 1) * CHUNK
    merge_repeats(d_head, 0, head_row[step, 0:1, at:at + LANES], m_split, grads, at)
    c0.wait_recv()
    rel_half[...] = (rel_acc[mine, :] + rel_got[...]).astype(BF16)
    first, last = pl.ds(0, qrows), pl.ds(qrows, qrows)
    c1 = copy_to(rel_half.at[first], rel_got1.at[first], r_ss.at[1], r_rs.at[1], x_mate)
    c2 = copy_to(rel_half.at[last], rel_got1.at[last], r_ss.at[2], r_rs.at[2], y_mate)
    c1.start()
    c2.start()
    for p in range(1, CHUNK // LANES):
        at = (chunks - 1) * CHUNK + p * LANES
        merge_repeats(d_head, p * LANES, head_row[step, 0:1, at:at + LANES], m_split, grads, at)
    c1.wait_recv()
    rel_two[first, :] = (rel_half[first, :].astype(F32) + rel_got1[first, :].astype(F32)).astype(BF16)
    c3 = copy_to(rel_two.at[first], rel_got2.at[first], r_ss.at[3], r_rs.at[3], y_mate)
    c3.start()
    c2.wait_recv()
    rel_two[last, :] = (rel_half[last, :].astype(F32) + rel_got1[last, :].astype(F32)).astype(BF16)
    c4 = copy_to(rel_two.at[last], rel_got2.at[last], r_ss.at[4], r_rs.at[4], x_mate)
    c4.start()
    c3.wait_recv()
    c4.wait_recv()
    rel_sum[mine, :] = rel_two[...].astype(F32) + rel_got2[...].astype(F32)
    c5 = copy_to(rel_sum.at[mine], rel_sum.at[mine], r_ss.at[5], r_rs.at[5], mate)
    c5.start()
    loss_copy.wait_recv()
    loss_out[...] = loss_in[...] + jnp.where(lane_iota(8) == step, loss_recv[...] * (1.0 / edges), 0.0)
    c5.wait_recv()

    def rel_step(j, carry):
        at = pl.ds(pl.multiple_of(j * SUB, SUB), SUB)
        new = updated([rel_in[at, cols_of(c)] for c in range(4)], [rel_sum[at, cols_of(c)] for c in range(4)], emb_dim, lane)
        for c in range(4):
            rel_out[at, cols_of(c)] = new[c]
        return carry

    lax.fori_loop(0, REL_ROWS // SUB, rel_step, 0)
    for copy in q_copies + d_copies + [loss_copy, c0, c1, c2, c3, c4, c5]:
        copy.wait_send()


def scatter_kernel(step, emb_dim, head_hbm, tail_hbm, neg_hbm, grads, ent_in, ent, acc, head_idx, tail_idx, neg_idx, sems):
    lists = ((head_hbm, head_idx), (tail_hbm, tail_idx), (neg_hbm, neg_idx))
    fetches = [pltpu.make_async_copy(src.at[step], dst, sems.at[k]) for k, (src, dst) in enumerate(lists)]
    for fetch in fetches:
        fetch.start()

    def clear(j, carry):
        acc[pl.ds(pl.multiple_of(j * 512, 512), 512), :] = jnp.zeros((512, LANES), F32)
        return carry

    lax.fori_loop(0, acc.shape[0] // 512, clear, 0)
    base = 0
    for fetch, (_, idx) in zip(fetches, lists):
        fetch.wait()

        def block(j, carry, idx=idx, base=base):
            at = j * SUB
            rows = [row_of(idx[0, at + i]) for i in range(SUB)]
            new = [acc[rows[i], :] + grads[row_of(base + at + i), :] for i in range(SUB)]
            for i in range(SUB):
                acc[rows[i], :] = new[i]
            return carry

        lax.fori_loop(0, idx.shape[1] // SUB, block, 0)
        base += idx.shape[1]
    dense_update(ent, acc, 0, ent.shape[0] // (4 * SUB), emb_dim)


def swap_kernel(devs, tail, neg, mask, tail_got, neg_got, mask_got, ss, rs):
    me = lax.axis_index("ent")
    barrier = pltpu.get_barrier_semaphore()
    for d in range(1, devs):
        pl.semaphore_signal(barrier, inc=1, device_id={"ent": lax.rem(me + d, devs)}, device_id_type=pl.DeviceIdType.MESH)
    pl.semaphore_wait(barrier, devs - 1)
    copies = []
    for s in range(tail.shape[0]):
        owner = lax.rem(me + s + 1, devs)
        for k, (src, dst) in enumerate(((tail, tail_got), (neg, neg_got), (mask, mask_got))):
            copies.append(pltpu.make_async_remote_copy(src_ref=src.at[s], dst_ref=dst.at[s], send_sem=ss.at[s, k], recv_sem=rs.at[s, k],
                                                       device_id={"ent": owner}, device_id_type=pl.DeviceIdType.MESH))
            copies[-1].start()
    for copy in copies:
        copy.wait()


def enter_kernel(table, state, rel, ent, rel_out, loss_out, pad):
    blk = pl.program_id(0)
    cols = table.shape[1]
    half = table.shape[0] // 2
    short = half - LANES

    def piece(src, c, lanes, extra=None):
        first = (c // 2) * half
        width = lanes.stop - lanes.start
        if c % 2 == 0 and width == LANES:
            return src[first:first + LANES, lanes]
        count = LANES if c % 2 == 0 else short
        pad[...] = jnp.zeros((LANES, LANES), F32)
        pad[0:count, 0:width] = src[first + LANES * (c % 2):first + LANES * (c % 2) + count, lanes]
        if extra is not None:
            pad[LANES - 1:LANES, :] = extra
        return pad[...]

    @pl.when(blk == 0)
    def _():
        loss_out[...] = jnp.zeros_like(loss_out)
        count = rel.shape[1]
        for p in range(REL_ROWS // LANES):
            for c in range(4):
                rel_out[LANES * p:LANES * (p + 1), cols_of(c)] = jnp.transpose(piece(rel, c, slice(LANES * p, min(LANES * (p + 1), count))))

    for j in range(cols // LANES):
        lanes = slice(LANES * j, LANES * (j + 1))
        here = pieces(pl.multiple_of(blk * cols + j * LANES, LANES), LANES)
        for c in range(4):
            ent[here[c], :] = jnp.transpose(piece(table, c, lanes, state[j:j + 1, :] if c == 1 else None))


def leave_kernel(emb_dim, ent, rel, loss, table, state, rel_out, loss_out):
    blk = pl.program_id(0)
    cols = table.shape[1]
    half = emb_dim // 2
    short = half - LANES
    count = rel_out.shape[1]

    def put(dst, c, lanes, x):
        first = (c // 2) * half + LANES * (c % 2)
        rows = short if c % 2 else LANES
        dst[first:first + rows, lanes] = x[0:rows, 0:lanes.stop - lanes.start]

    @pl.when(blk == 0)
    def _():
        loss_out[...] = loss[...]
        for p in range(REL_ROWS // LANES):
            for c in range(4):
                put(rel_out, c, slice(LANES * p, min(LANES * (p + 1), count)), jnp.transpose(rel[LANES * p:LANES * (p + 1), cols_of(c)]))

    for j in range(cols // LANES):
        at = pl.multiple_of(blk * cols + j * LANES, LANES)
        lanes = slice(LANES * j, LANES * (j + 1))
        here = pieces(at, LANES)
        for c in range(4):
            turned = jnp.transpose(ent[here[c], :])
            put(table, c, lanes, turned)
            if c == 1:
                state[j:j + 1, :] = turned[LANES - 1:LANES, :]


def solution(mesh):
    devs = mesh.shape["ent"]
    row_spec = P(("sweep", "ent"), None)
    state_spec = P(("sweep", "ent"))
    rel_spec = P("sweep", None)
    edge_spec = P(("sweep", "ent"), None, None)
    in_vmem = pl.BlockSpec(memory_space=VMEM)
    in_smem = pl.BlockSpec(memory_space=SMEM)
    in_any = pl.BlockSpec(memory_space=pl.ANY)
    hold = lambda x: pltpu.with_memory_space_constraint(x, VMEM)
    DMA = pltpu.SemaphoreType.DMA

    def per_device(ent_part, ada_part, rel_table, head_idx, tail_idx, rel_idx, neg_idx, edge_mask):
        rows, emb_dim = ent_part.shape
        rounds, edges = head_idx.shape[1:]
        negs = neg_idx.shape[2]
        chunks = edges // CHUNK
        total = 2 * edges + negs
        table_vmem = VMEM((rows * 4, LANES), F32)
        rel_vmem = VMEM((REL_ROWS, 4 * LANES), F32)
        loss_vmem = VMEM((8, LANES), F32)
        block = min(1024, rows)
        by_round = lambda x: x.transpose(1, 0, 2)
        head_idx, tail_idx, rel_idx, neg_idx, edge_mask = map(by_round, (head_idx, tail_idx, rel_idx, neg_idx, edge_mask))
        table_spec = pl.BlockSpec((emb_dim, block), lambda i: (0, i))
        ada_spec = pl.BlockSpec((block // LANES, LANES), lambda i: (i, 0))

        tail_got, neg_got, mask_got = pl.pallas_call(
            functools.partial(swap_kernel, devs),
            out_shape=tuple(jax.ShapeDtypeStruct(x.shape, x.dtype) for x in (tail_idx, neg_idx, edge_mask)),
            in_specs=[in_any] * 3,
            out_specs=(in_any,) * 3,
            scratch_shapes=[DMA((rounds, 3)), DMA((rounds, 3))],
            compiler_params=pltpu.CompilerParams(collective_id=rounds, has_side_effects=True, vmem_limit_bytes=1 << 20),
            name="swap",
        )(tail_idx, neg_idx, edge_mask)
        ent, rel, loss = pl.pallas_call(
            enter_kernel,
            grid=(rows // block,),
            out_shape=(table_vmem, rel_vmem, loss_vmem),
            in_specs=[table_spec, ada_spec, in_vmem],
            out_specs=(in_vmem,) * 3,
            scratch_shapes=[VMEM((LANES, LANES), F32)],
            compiler_params=pltpu.CompilerParams(vmem_limit_bytes=25 << 20),
            name="enter",
        )(ent_part.T, ada_part.reshape(rows // LANES, LANES), rel_table.T)

        wire = VMEM((chunks, 3 * CHUNK + SUB, LANES), BF16)
        full = VMEM((edges, 4 * LANES), F32)
        some = VMEM((CHUNK, 4 * LANES), F32)
        half_rel = (REL_ROWS // 2, 4 * LANES)
        lists = [SMEM((1, edges), jnp.int32), SMEM((1, edges), jnp.int32), SMEM((1, negs), jnp.int32)]
        for step in range(rounds):
            grads, rel, loss = pl.pallas_call(
                functools.partial(main_kernel, step, devs, emb_dim),
                out_shape=(VMEM((total * 4, LANES), F32), rel_vmem, loss_vmem),
                in_specs=[in_smem] * 3 + [in_vmem] * 8,
                out_specs=(in_vmem,) * 3,
                scratch_shapes=[
                    VMEM((4 * SUB, LANES), F32), VMEM((REL_ROWS, 12 * LANES), BF16), full, full,
                    VMEM((edges + negs, 4 * LANES), BF16), wire, wire, wire, wire,
                    VMEM((CHUNK, 4 * LANES), BF16), VMEM((CHUNK, LANES), F32), VMEM((CHUNK, negs), F32),
                    VMEM((CHUNK, 1), F32), VMEM((CHUNK, 1), F32), VMEM((CHUNK, negs), BF16), some,
                    VMEM((edges + negs, 4 * LANES), F32), some, VMEM((CHUNK, 12 * LANES), BF16), VMEM((LANES, 12 * LANES), BF16),
                    VMEM((REL_ROWS, 4 * LANES), F32), VMEM(half_rel, F32), VMEM(half_rel, BF16), VMEM(half_rel, BF16), VMEM(half_rel, BF16), VMEM(half_rel, BF16),
                    VMEM((REL_ROWS, 4 * LANES), F32), VMEM((8, LANES), F32), VMEM((8, LANES), F32),
                ] + [DMA((chunks,))] * 4 + [DMA((7,))] * 2,
                compiler_params=pltpu.CompilerParams(collective_id=step, has_side_effects=True, vmem_limit_bytes=25 << 20),
                name="train",
            )(head_idx, tail_got, neg_got, head_idx, tail_got, neg_got, mask_got, rel_idx, hold(loss), hold(rel), hold(ent.reshape(rows, 4, LANES)))
            ent = pl.pallas_call(
                functools.partial(scatter_kernel, step, emb_dim),
                out_shape=table_vmem,
                in_specs=[in_any] * 3 + [in_vmem] * 2,
                out_specs=in_vmem,
                input_output_aliases={4: 0},
                scratch_shapes=[VMEM((rows * 4, LANES), F32)] + lists + [DMA((3,))],
                compiler_params=pltpu.CompilerParams(vmem_limit_bytes=18 << 20),
                name="scatter",
            )(head_idx, tail_got, neg_got, hold(grads), hold(ent))

        table_t, state, rel_t, loss = pl.pallas_call(
            functools.partial(leave_kernel, emb_dim),
            grid=(rows // block,),
            out_shape=(jax.ShapeDtypeStruct((emb_dim, rows), F32), jax.ShapeDtypeStruct((rows // LANES, LANES), F32),
                       jax.ShapeDtypeStruct(rel_table.T.shape, F32), jax.ShapeDtypeStruct((8, LANES), F32)),
            in_specs=[in_vmem] * 3,
            out_specs=(table_spec, ada_spec, in_vmem, in_vmem),
            compiler_params=pltpu.CompilerParams(vmem_limit_bytes=25 << 20),
            name="leave",
        )(hold(ent), hold(rel), hold(loss))
        return table_t.T, state.reshape(rows), rel_t.T, loss[0:1, 0:rounds]

    return jax.shard_map(per_device, mesh=mesh, in_specs=(row_spec, state_spec, rel_spec, edge_spec, edge_spec, edge_spec, edge_spec, edge_spec), out_specs=(row_spec, state_spec, rel_spec, row_spec), check_vma=False)
```

time: 925 us -> 508 us (0.55)
  Pallas kernels: 806 us -> 493 us
  local copies, waits for them, and re-layouts: 92.5 us -> 4.44 us
    pallas_call x12 -> x13, Pallas kernels: 756 us -> 476 us  [the longest x6 355 us: per_device(): pl.pallas_call(functools.partial(main_kernel, step, devs, emb_dim), out_s...]
    unnamed x79 -> x14, local copies, waits for them, and re-layouts: 68.1 us -> 3.93 us
    pallas_call x1, Pallas kernels: 30.7 us -> 7.93 us  [per_device(): pl.pallas_call(functools.partial(leave_kernel, emb_dim), grid=(rows // bl...]
    slice x20 -> x1, local copies, waits for them, and re-layouts: 12.2 us -> 0.51 us  [per_device(): return (table_t.T, state.reshape(rows), rel_t.T, loss[0:1, 0:rounds])]
    pallas_call x1, Pallas kernels: 19.3 us -> 9.4 us  [per_device(): pl.pallas_call(enter_kernel, grid=(rows // block,), out_shape=(table_vmem...]
  transfers between devices with their start and end apart: 6 -> 0, of which waited for: 1 -> 0; matrix products, arithmetic and copies ran while one was open for 1% -> 0% of each run, Pallas kernels for 2% -> 0%
where the time goes in v2:
time: 508 us; the launch traced here: 499 us
  Pallas kernels  493 us (97%)
    pallas_call x6, Pallas kernels, per_device(): pl.pallas_call(functools.partial(main_kernel, step, devs, emb_dim), out_s...  355 us
    pallas_call x6, Pallas kernels, per_device(): pl.pallas_call(functools.partial(scatter_kernel, step, emb_dim), out_shap...  114 us

profile of v2, /device:TPU:1, one launch (start us, length us, event | category | flops | bytes accessed | tf_op | source)
XLA Modules:
  0.0 498.9 jit_solution(14687439149442309763)
XLA Ops:
  0.6 0.0 copy-start
  0.6 0.0 copy-start.1
  0.7 0.0 copy-start.4
  0.7 0.7 copy-done.4
  1.4 0.0 copy-start.5
  1.4 0.7 copy-done.5
  2.1 0.0 copy-start.6
  2.1 0.7 copy-done.6
  2.8 6.3 %swap.1 = (s32[6,1,1024]{2,1,0:T(1,128)S(1)}, s32[6,1,256]{2,1,0:T(1,128)S(1)}, s32[6,1,1024]{2,1,0:T(1,128)S(1)}) custom-call(s32[6,1,1024]{2,1,0:T(1,128)S(1)} %bitcast.49, s32[6,1,256]{2,1,0:T(1,128)S(1)} %bitcast.51, s32[6,1,1024]{2,1,0:T(1,128)S(1)} %bitcast.50), custom_call_target="tpu_custom_call" | custom-call | tf_op jit(solution)/shard_map/swap/pallas_call | solution.py:484
  9.1 0.0 copy-start.2
  9.2 1.0 copy-done.2
  10.1 0.0 copy-start.3
  10.1 0.8 copy-done.3
  10.9 9.4 %enter.1 = (f32[32768,128]{1,0:T(8,128)S(1)}, f32[256,512]{1,0:T(8,128)S(1)}, f32[8,128]{1,0:T(8,128)S(1)}) custom-call(f32[400,8192]{1,0:T(8,128)} %bitcast.52, f32[64,128]{1,0:T(8,128)S(1)} %bitcast.48, f32[400,237]{1,0:T(8,128)S(1)} %bitcast.47), custom_call_target="tpu_custom_call" | custom-call | tf_op jit(solution)/shard_map/enter/pallas_call | solution.py:493
  20.3 0.0 copy-done
  20.3 0.0 copy-done.1
  20.3 56.8 %train.6 = (f32[9216,128]{1,0:T(8,128)S(1)}, f32[256,512]{1,0:T(8,128)S(1)}, f32[8,128]{1,0:T(8,128)S(1)}) custom-call(s32[6,1,1024]{2,1,0:T(1,128)S(1)} %bitcast.23, s32[6,1,1024]{2,1,0:T(1,128)S(1)} %get-tuple-element.32.tail_idx.tail_row.tail_hbm, s32[6,1,256]{2,1,0:T(1,128)S(1)} %get-tuple-element.33.neg_idx.neg_row.neg_hbm, s32[6,1,1024]{2,1,0:T(1,128)S(1)} %bitcast.24, ...), custom_call_target="tpu_custom_call" | custom-call | tf_op jit(solution)/shard_map/train/pallas_call | solution.py:510
  77.1 19.0 %scatter.6.ent_in = f32[32768,128]{1,0:T(8,128)S(1)} custom-call(s32[6,1,1024]{2,1,0:T(1,128)S(1)} %bitcast.25, s32[6,1,1024]{2,1,0:T(1,128)S(1)} %get-tuple-element.32.tail_idx.tail_row.tail_hbm, s32[6,1,256]{2,1,0:T(1,128)S(1)} %get-tuple-element.33.neg_idx.neg_row.neg_hbm, ...), custom_call_target="tpu_custom_call", output_to_operand_aliasing={{}: (4, {})} | custom-call | tf_op jit(solution)/shard_map/scatter/pallas_call | solution.py:527
  96.2 58.7 %train.7 = (f32[9216,128]{1,0:T(8,128)S(1)}, f32[256,512]{1,0:T(8,128)S(1)}, f32[8,128]{1,0:T(8,128)S(1)}) custom-call(s32[6,1,1024]{2,1,0:T(1,128)S(1)} %bitcast.26, s32[6,1,1024]{2,1,0:T(1,128)S(1)} %get-tuple-element.32.tail_idx.tail_row.tail_hbm, s32[6,1,256]{2,1,0:T(1,128)S(1)} %get-tuple-element.33.neg_idx.neg_row.neg_hbm, s32[6,1,1024]{2,1,0:T(1,128)S(1)} %bitcast.27, ...), custom_call_target="tpu_custom_call" | custom-call | tf_op jit(solution)/shard_map/train/pallas_call | solution.py:510
  154.9 19.0 %scatter.7.ent_in = f32[32768,128]{1,0:T(8,128)S(1)} custom-call(s32[6,1,1024]{2,1,0:T(1,128)S(1)} %bitcast.28, s32[6,1,1024]{2,1,0:T(1,128)S(1)} %get-tuple-element.32.tail_idx.tail_row.tail_hbm, s32[6,1,256]{2,1,0:T(1,128)S(1)} %get-tuple-element.33.neg_idx.neg_row.neg_hbm, ...), custom_call_target="tpu_custom_call", output_to_operand_aliasing={{}: (4, {})} | custom-call | tf_op jit(solution)/shard_map/scatter/pallas_call | solution.py:527
  173.9 61.4 %train.8 = (f32[9216,128]{1,0:T(8,128)S(1)}, f32[256,512]{1,0:T(8,128)S(1)}, f32[8,128]{1,0:T(8,128)S(1)}) custom-call(s32[6,1,1024]{2,1,0:T(1,128)S(1)} %bitcast.29, s32[6,1,1024]{2,1,0:T(1,128)S(1)} %get-tuple-element.32.tail_idx.tail_row.tail_hbm, s32[6,1,256]{2,1,0:T(1,128)S(1)} %get-tuple-element.33.neg_idx.neg_row.neg_hbm, s32[6,1,1024]{2,1,0:T(1,128)S(1)} %bitcast.30, ...), custom_call_target="tpu_custom_call" | custom-call | tf_op jit(solution)/shard_map/train/pallas_call | solution.py:510
  235.3 19.0 %scatter.8.ent_in = f32[32768,128]{1,0:T(8,128)S(1)} custom-call(s32[6,1,1024]{2,1,0:T(1,128)S(1)} %bitcast.31, s32[6,1,1024]{2,1,0:T(1,128)S(1)} %get-tuple-element.32.tail_idx.tail_row.tail_hbm, s32[6,1,256]{2,1,0:T(1,128)S(1)} %get-tuple-element.33.neg_idx.neg_row.neg_hbm, ...), custom_call_target="tpu_custom_call", output_to_operand_aliasing={{}: (4, {})} | custom-call | tf_op jit(solution)/shard_map/scatter/pallas_call | solution.py:527
  254.4 58.8 %train.9 = (f32[9216,128]{1,0:T(8,128)S(1)}, f32[256,512]{1,0:T(8,128)S(1)}, f32[8,128]{1,0:T(8,128)S(1)}) custom-call(s32[6,1,1024]{2,1,0:T(1,128)S(1)} %bitcast.32, s32[6,1,1024]{2,1,0:T(1,128)S(1)} %get-tuple-element.32.tail_idx.tail_row.tail_hbm, s32[6,1,256]{2,1,0:T(1,128)S(1)} %get-tuple-element.33.neg_idx.neg_row.neg_hbm, s32[6,1,1024]{2,1,0:T(1,128)S(1)} %bitcast.33, ...), custom_call_target="tpu_custom_call" | custom-call | tf_op jit(solution)/shard_map/train/pallas_call | solution.py:510
  313.2 19.0 %scatter.9.ent_in = f32[32768,128]{1,0:T(8,128)S(1)} custom-call(s32[6,1,1024]{2,1,0:T(1,128)S(1)} %bitcast.34, s32[6,1,1024]{2,1,0:T(1,128)S(1)} %get-tuple-element.32.tail_idx.tail_row.tail_hbm, s32[6,1,256]{2,1,0:T(1,128)S(1)} %get-tuple-element.33.neg_idx.neg_row.neg_hbm, ...), custom_call_target="tpu_custom_call", output_to_operand_aliasing={{}: (4, {})} | custom-call | tf_op jit(solution)/shard_map/scatter/pallas_call | solution.py:527
  332.3 60.9 %train.10 = (f32[9216,128]{1,0:T(8,128)S(1)}, f32[256,512]{1,0:T(8,128)S(1)}, f32[8,128]{1,0:T(8,128)S(1)}) custom-call(s32[6,1,1024]{2,1,0:T(1,128)S(1)} %bitcast.35, s32[6,1,1024]{2,1,0:T(1,128)S(1)} %get-tuple-element.32.tail_idx.tail_row.tail_hbm, s32[6,1,256]{2,1,0:T(1,128)S(1)} %get-tuple-element.33.neg_idx.neg_row.neg_hbm, ...), custom_call_target="tpu_custom_call" | custom-call | tf_op jit(solution)/shard_map/train/pallas_call | solution.py:510
  393.2 19.0 %scatter.10.ent_in = f32[32768,128]{1,0:T(8,128)S(1)} custom-call(s32[6,1,1024]{2,1,0:T(1,128)S(1)} %bitcast.37, s32[6,1,1024]{2,1,0:T(1,128)S(1)} %get-tuple-element.32.tail_idx.tail_row.tail_hbm, s32[6,1,256]{2,1,0:T(1,128)S(1)} %get-tuple-element.33.neg_idx.neg_row.neg_hbm, ...), custom_call_target="tpu_custom_call", output_to_operand_aliasing={{}: (4, {})} | custom-call | tf_op jit(solution)/shard_map/scatter/pallas_call | solution.py:527
  412.3 58.7 %train.11 = (f32[9216,128]{1,0:T(8,128)S(1)}, f32[256,512]{1,0:T(8,128)S(1)}, f32[8,128]{1,0:T(8,128)S(1)}) custom-call(s32[6,1,1024]{2,1,0:T(1,128)S(1)} %bitcast.38, s32[6,1,1024]{2,1,0:T(1,128)S(1)} %get-tuple-element.32.tail_idx.tail_row.tail_hbm, s32[6,1,256]{2,1,0:T(1,128)S(1)} %get-tuple-element.33.neg_idx.neg_row.neg_hbm, ...), custom_call_target="tpu_custom_call" | custom-call | tf_op jit(solution)/shard_map/train/pallas_call | solution.py:510
  471.0 19.0 %scatter.11.ent = f32[32768,128]{1,0:T(8,128)S(1)} custom-call(s32[6,1,1024]{2,1,0:T(1,128)S(1)} %bitcast.40, s32[6,1,1024]{2,1,0:T(1,128)S(1)} %get-tuple-element.32.tail_idx.tail_row.tail_hbm, s32[6,1,256]{2,1,0:T(1,128)S(1)} %get-tuple-element.33.neg_idx.neg_row.neg_hbm, f32[9216,128]{1,0:T(8,128)S(1)} %get-tuple-element.53.grads, ...), custom_call_target="tpu_custom_call", output_to_operand_aliasing={{}: (4, {})} | custom-call | tf_op jit(solution)/shard_map/scatter/pallas_call | solution.py:527
  490.1 7.9 %leave.1 = (f32[400,8192]{1,0:T(8,128)}, f32[64,128]{1,0:T(8,128)}, f32[400,237]{1,0:T(8,128)}, f32[8,128]{1,0:T(8,128)S(1)}) custom-call(f32[32768,128]{1,0:T(8,128)S(1)} %scatter.11.ent, f32[256,512]{1,0:T(8,128)S(1)} %get-tuple-element.54.rel, f32[8,128]{1,0:T(8,128)S(1)} %get-tuple-element.55.loss), custom_call_target="tpu_custom_call" | custom-call | tf_op jit(solution)/shard_map/leave/pallas_call | solution.py:538
  498.0 0.5 slice.3
Async XLA Ops:
  0.6 19.7 %copy-start = (s32[1,6,1024]{2,0,1:T(1,128)S(1)}, s32[1,6,1024]{2,0,1:T(1,128)}, u32[]{:S(2)}) copy-start(s32[1,6,1024]{2,0,1:T(1,128)} %param.11) | copy-start | bytes 73732
  0.6 19.7 %copy-start.1 = (s32[1,6,1024]{2,0,1:T(1,128)S(1)}, s32[1,6,1024]{2,0,1:T(1,128)}, u32[]{:S(2)}) copy-start(s32[1,6,1024]{2,0,1:T(1,128)} %param.13) | copy-start | bytes 73732
  0.7 0.8 copy-start.4
  1.4 0.7 copy-start.5
  2.1 0.7 copy-start.6
  9.1 1.0 copy-start.2
  10.1 0.8 copy-start.3
